TPU v7x, 128 devices: a whole 4x4x4 slice. The times are simulated.
128 devices in a mesh: data: 64 (over z, y, x), model: 2 (over core).
Axes of the slice: x: 4, y: 4, z: 4, core: 2. Of those that a mesh axis runs over, the one named last changes fastest.
Arguments:
- x_t: bfloat16 [128, 128, 768], P('data', 'model')
- x_s: bfloat16 [128, 128, 312], P(('data', 'model'))
- lengths: int32 [128], P(('data', 'model'))
- t_w1: bfloat16 [48, 768, 3072], P(None, None, 'model')
- t_w2: bfloat16 [48, 3072, 768], P(None, 'model')
- t_gain: float32 [48, 768], replicated
- s_w1: bfloat16 [6, 312, 1248], replicated
- s_w2: bfloat16 [6, 1248, 312], replicated
- s_gain1: float32 [6, 312], replicated
- s_gain2: float32 [6, 312], replicated
- s_proj: bfloat16 [6, 312, 768], replicated
Outputs:
- output 1: float32 [], replicated
- output 2: float32 [6, 312, 1248], replicated
- output 3: float32 [6, 1248, 312], replicated
- output 4: float32 [6, 312], replicated
- output 5: float32 [6, 312], replicated
- output 6: float32 [6, 312, 768], replicated
All inputs are finite; a program needn't handle non-finite values.
Results may differ from a plain program's by a relative error of at most 0.00589431.
Values are sent between devices in bfloat16 or wider.
A program may use at most 1 GiB of HBM per device.

v0:
```python
import jax
import jax.numpy as jnp
from jax import lax
from jax.sharding import PartitionSpec as P

RMS_EPS = 1e-6
ALL_AXES = ('data', 'model')


def rms_gain(hidden, gain):
    wide = hidden.astype(jnp.float32)
    return wide * lax.rsqrt(jnp.mean(wide * wide, axis=-1, keepdims=True) + RMS_EPS) * gain


def teacher_layer(hidden, w_in, w_out, gain):
    normed = rms_gain(hidden, gain).astype(jnp.bfloat16)
    gathered = lax.all_gather(normed, 'model', axis=1, tiled=True)
    activated = jax.nn.gelu(jnp.einsum('bsd,df->bsf', gathered, w_in, preferred_element_type=jnp.float32)).astype(jnp.bfloat16)
    partial_out = jnp.einsum('bsf,fd->bsd', activated, w_out, preferred_element_type=jnp.float32)
    update = lax.psum_scatter(partial_out, 'model', scatter_dimension=1, tiled=True)
    return (hidden.astype(jnp.float32) + update).astype(jnp.bfloat16)


def student_grads(x_s, lengths, features, s_w1, s_w2, s_gain1, s_gain2, s_proj, t_width):
    s_layers = s_w1.shape[0]
    valid = (jnp.arange(x_s.shape[1])[None, :] < lengths[:, None]).astype(jnp.float32)[:, :, None]
    count = lax.psum(jnp.sum(lengths).astype(jnp.float32), ALL_AXES)
    err_scale = 2.0 / (s_layers * t_width * count)
    wide_state = x_s.astype(jnp.float32)
    saved = []
    proj_grads = []
    gain_out_grads = []
    sq_sum = jnp.zeros((), jnp.float32)
    for layer_idx in range(s_layers):
        normed_wide, norm_in_vjp = jax.vjp(rms_gain, wide_state, s_gain1[layer_idx])
        normed = normed_wide.astype(jnp.bfloat16)
        pre_act = jnp.einsum('bsd,df->bsf', normed, s_w1[layer_idx], preferred_element_type=jnp.float32)
        act_wide, gelu_vjp = jax.vjp(jax.nn.gelu, pre_act)
        activated = act_wide.astype(jnp.bfloat16)
        update = jnp.einsum('bsf,fd->bsd', activated, s_w2[layer_idx], preferred_element_type=jnp.float32)
        wide_state = (wide_state + update).astype(jnp.bfloat16).astype(jnp.float32)
        out_wide, norm_out_vjp = jax.vjp(rms_gain, wide_state, s_gain2[layer_idx])
        normed_out = out_wide.astype(jnp.bfloat16)
        projected = jnp.einsum('bsd,dt->bst', normed_out, s_proj[layer_idx], preferred_element_type=jnp.float32)
        errors = (projected - features[layer_idx].astype(jnp.float32)) * valid
        sq_sum = sq_sum + jnp.sum(errors * errors)
        d_err = (errors * err_scale).astype(jnp.bfloat16)
        proj_grads.append(jnp.einsum('bsd,bst->dt', normed_out, d_err, preferred_element_type=jnp.float32))
        d_normed_out = jnp.einsum('bst,dt->bsd', d_err, s_proj[layer_idx], preferred_element_type=jnp.float32)
        d_state_proj, d_gain_out = norm_out_vjp(d_normed_out)
        gain_out_grads.append(d_gain_out)
        saved.append((normed, activated, gelu_vjp, norm_in_vjp, d_state_proj))
    w_in_grads = []
    w_out_grads = []
    gain_in_grads = []
    d_state = jnp.zeros(x_s.shape, jnp.float32)
    for layer_idx in reversed(range(s_layers)):
        normed, activated, gelu_vjp, norm_in_vjp, d_state_proj = saved[layer_idx]
        d_state = d_state + d_state_proj
        d_update = d_state.astype(jnp.bfloat16)
        w_out_grads.append(jnp.einsum('bsf,bsd->fd', activated, d_update, preferred_element_type=jnp.float32))
        d_act = jnp.einsum('bsd,fd->bsf', d_update, s_w2[layer_idx], preferred_element_type=jnp.float32)
        d_pre = gelu_vjp(d_act)[0].astype(jnp.bfloat16)
        w_in_grads.append(jnp.einsum('bsd,bsf->df', normed, d_pre, preferred_element_type=jnp.float32))
        d_normed = jnp.einsum('bsf,df->bsd', d_pre, s_w1[layer_idx], preferred_element_type=jnp.float32)
        d_state_norm, d_gain_in = norm_in_vjp(d_normed)
        gain_in_grads.append(d_gain_in)
        d_state = d_state + d_state_norm
    local_sums = (sq_sum * err_scale * 0.5, jnp.stack(w_in_grads[::-1]), jnp.stack(w_out_grads[::-1]),
                  jnp.stack(gain_in_grads[::-1]), jnp.stack(gain_out_grads), jnp.stack(proj_grads))
    return lax.psum(local_sums, ALL_AXES)


def solution(mesh):
    def body(x_t, x_s, lengths, t_w1, t_w2, t_gain, s_w1, s_w2, s_gain1, s_gain2, s_proj):
        per_group = t_w1.shape[0] // s_w1.shape[0]
        hidden = x_t
        features = []
        for layer_idx in range(t_w1.shape[0]):
            hidden = teacher_layer(hidden, t_w1[layer_idx], t_w2[layer_idx], t_gain[layer_idx])
            if (layer_idx + 1) % per_group == 0:
                features.append(lax.all_to_all(hidden, 'model', 0, 1, tiled=True))
        return student_grads(x_s, lengths, features, s_w1, s_w2, s_gain1, s_gain2, s_proj, x_t.shape[2])

    in_specs = (P('data', 'model', None), P(ALL_AXES, None, None), P(ALL_AXES),
                P(None, None, 'model'), P(None, 'model', None), P(), P(), P(), P(), P(), P())
    out_specs = (P(), P(), P(), P(), P(), P())
    return jax.shard_map(body, mesh=mesh, in_specs=in_specs, out_specs=out_specs, check_vma=False)
```

profile of v0, /device:TPU:1, one launch (start us, length us, event | category | flops | bytes accessed | tf_op | source)
XLA Modules:
  0.0 1380.5 jit_solution(11851321160952486945)
XLA Ops:
  18.5 13.6 reduce-scatter.49.cloned.1.call-done
  40.3 12.3 reduce-scatter.51.cloned.1.call-done
  60.9 12.3 reduce-scatter.53.cloned.1.call-done
  81.4 12.2 reduce-scatter.55.cloned.1.call-done
  101.9 12.3 reduce-scatter.57.cloned.1.call-done
  122.4 12.2 reduce-scatter.59.cloned.1.call-done
  142.9 12.3 reduce-scatter.61.cloned.1.call-done
  163.6 12.2 reduce-scatter.63.cloned.1.call-done
  184.1 12.3 reduce-scatter.65.cloned.1.call-done
  205.3 11.6 reduce-scatter.67.cloned.1.call-done
  225.2 12.3 reduce-scatter.69.cloned.1.call-done
  245.7 12.2 reduce-scatter.71.cloned.1.call-done
  266.2 12.3 reduce-scatter.73.cloned.1.call-done
  286.7 12.2 reduce-scatter.75.cloned.1.call-done
  307.4 12.3 reduce-scatter.77.cloned.1.call-done
  328.0 12.2 reduce-scatter.79.cloned.1.call-done
  348.5 12.3 reduce-scatter.81.cloned.1.call-done
  369.0 12.2 reduce-scatter.83.cloned.1.call-done
  389.5 12.3 reduce-scatter.85.cloned.1.call-done
  410.0 12.2 reduce-scatter.87.cloned.1.call-done
  430.5 12.3 reduce-scatter.89.cloned.1.call-done
  451.4 12.2 reduce-scatter.91.cloned.1.call-done
  471.9 12.3 reduce-scatter.93.cloned.1.call-done
  492.5 12.2 reduce-scatter.95.cloned.1.call-done
  513.0 12.3 reduce-scatter.97.cloned.1.call-done
  533.5 12.2 reduce-scatter.99.cloned.1.call-done
  554.0 12.3 reduce-scatter.101.cloned.1.call-done
  575.2 11.6 reduce-scatter.103.cloned.1.call-done
  595.2 12.3 reduce-scatter.105.cloned.1.call-done
  615.7 12.2 reduce-scatter.107.cloned.1.call-done
  636.2 12.3 reduce-scatter.109.cloned.1.call-done
  656.7 12.2 reduce-scatter.111.cloned.1.call-done
  677.2 12.3 reduce-scatter.113.cloned.1.call-done
  697.8 12.2 reduce-scatter.115.cloned.1.call-done
  718.3 12.3 reduce-scatter.117.cloned.1.call-done
  739.0 12.2 reduce-scatter.119.cloned.1.call-done
  759.5 12.3 reduce-scatter.121.cloned.1.call-done
  780.0 12.2 reduce-scatter.123.cloned.1.call-done
  800.5 12.3 reduce-scatter.125.cloned.1.call-done
  821.1 12.2 reduce-scatter.127.cloned.1.call-done
  841.6 12.2 reduce-scatter.129.cloned.1.call-done
  862.1 12.2 reduce-scatter.131.cloned.1.call-done
  883.0 12.2 reduce-scatter.133.cloned.1.call-done
  907.9 7.9 reduce-scatter.135.cloned.1.call-done
  966.4 66.5 %psum.49 = f32[]{:T(128)} all-reduce(f32[]{:T(128)S(6)} %convert_element_type.1079), channel_id=1, replica_groups=mesh['data'=64,'model'=2] {'data','model'}, use_global_device_ids=true, to_apply=%region_109.0 | all-reduce | flops 1 | bytes 8 | tf_op jit(solution)/shard_map/psum | solution.py:27
  1136.7 64.1 %all-reduce = (f32[]{:T(128)}, f32[6,312]{1,0:T(8,128)}, f32[6,312]{1,0:T(8,128)}) all-reduce(f32[]{:T(128)S(6)} %mul.3285, f32[6,312]{1,0:T(8,128)S(1)} %stack.125, f32[6,312]{1,0:T(8,128)S(1)} %stack.132), channel_id=1, replica_groups=mesh['data'=64,'model'=2] {'data','model'}, use_global_device_ids=true, to_apply=%region_110.0 | all-reduce | flops 3745 | bytes 29960 | tf_op jit(solution)/shard_map/psum | solution.py:71
  1200.8 155.4 %all-reduce.4.cloned.1.call-done = (f32[6,312,1248]{2,1,0:T(8,128)}, f32[6,1248,312]{1,2,0:T(8,128)}, f32[6,312,768]{2,1,0:T(8,128)}) async-done(((f32[6,312,1248]{2,1,0:T(8,128)}, f32[6,1248,312]{1,2,0:T(8,128)}, f32[6,312,768]{2,1,0:T(8,128)}), (f32[6,312,1248]{2,1,0:T(8,128)}, f32[6,1248,312]{1,2,0:T(8,128)}, f32[6,312,768]{2,1,0:T(8,128)})) %all-reduce.4.cloned.1.call-update) | async-done | bytes 24440848 | tf_op jit(solution)/shard_map/psum | solution.py:71
  1356.1 9.4 copy.36
  (646 shorter events, 528.4 us)
Async XLA Ops:
  18.4 34.2 %reduce-scatter.51.cloned.1.call-start = ((), (), s32[]{:S(2)}) async-start(), calls=%async_computation.55 | async-start | bytes 1179648 | tf_op jit(solution)/shard_map/reduce_scatter | solution.py:20
  40.3 32.8 %reduce-scatter.53.cloned.1.call-start = ((), (), s32[]{:S(2)}) async-start(), calls=%async_computation.56 | async-start | bytes 1179648 | tf_op jit(solution)/shard_map/reduce_scatter | solution.py:20
  60.8 32.8 %reduce-scatter.55.cloned.1.call-start = ((), (), s32[]{:S(2)}) async-start(), calls=%async_computation.57 | async-start | bytes 1179648 | tf_op jit(solution)/shard_map/reduce_scatter | solution.py:20
  81.3 32.8 %reduce-scatter.57.cloned.1.call-start = ((), (), s32[]{:S(2)}) async-start(), calls=%async_computation.58 | async-start | bytes 1179648 | tf_op jit(solution)/shard_map/reduce_scatter | solution.py:20
  101.8 32.8 %reduce-scatter.59.cloned.1.call-start = ((), (), s32[]{:S(2)}) async-start(), calls=%async_computation.59 | async-start | bytes 1179648 | tf_op jit(solution)/shard_map/reduce_scatter | solution.py:20
  122.4 32.8 %reduce-scatter.61.cloned.1.call-start = ((), (), s32[]{:S(2)}) async-start(), calls=%async_computation.60 | async-start | bytes 1179648 | tf_op jit(solution)/shard_map/reduce_scatter | solution.py:20
  142.9 33.0 %reduce-scatter.63.cloned.1.call-start = ((), (), s32[]{:S(2)}) async-start(), calls=%async_computation.61 | async-start | bytes 1179648 | tf_op jit(solution)/shard_map/reduce_scatter | solution.py:20
  163.6 32.8 %reduce-scatter.65.cloned.1.call-start = ((), (), s32[]{:S(2)}) async-start(), calls=%async_computation.62 | async-start | bytes 1179648 | tf_op jit(solution)/shard_map/reduce_scatter | solution.py:20
  184.1 32.9 %reduce-scatter.67.cloned.1.call-start = ((), (), s32[]{:S(2)}) async-start(), calls=%async_computation.63 | async-start | bytes 1179648 | tf_op jit(solution)/shard_map/reduce_scatter | solution.py:20
  204.6 32.8 %reduce-scatter.69.cloned.1.call-start = ((), (), s32[]{:S(2)}) async-start(), calls=%async_computation.64 | async-start | bytes 1179648 | tf_op jit(solution)/shard_map/reduce_scatter | solution.py:20
  225.1 32.8 %reduce-scatter.71.cloned.1.call-start = ((), (), s32[]{:S(2)}) async-start(), calls=%async_computation.65 | async-start | bytes 1179648 | tf_op jit(solution)/shard_map/reduce_scatter | solution.py:20
  245.6 32.8 %reduce-scatter.73.cloned.1.call-start = ((), (), s32[]{:S(2)}) async-start(), calls=%async_computation.66 | async-start | bytes 1179648 | tf_op jit(solution)/shard_map/reduce_scatter | solution.py:20
  266.1 32.8 %reduce-scatter.75.cloned.1.call-start = ((), (), s32[]{:S(2)}) async-start(), calls=%async_computation.67 | async-start | bytes 1179648 | tf_op jit(solution)/shard_map/reduce_scatter | solution.py:20
  286.7 33.0 %reduce-scatter.77.cloned.1.call-start = ((), (), s32[]{:S(2)}) async-start(), calls=%async_computation.68 | async-start | bytes 1179648 | tf_op jit(solution)/shard_map/reduce_scatter | solution.py:20
  307.4 32.8 %reduce-scatter.79.cloned.1.call-start = ((), (), s32[]{:S(2)}) async-start(), calls=%async_computation.69 | async-start | bytes 1179648 | tf_op jit(solution)/shard_map/reduce_scatter | solution.py:20
  327.9 32.8 %reduce-scatter.81.cloned.1.call-start = ((), (), s32[]{:S(2)}) async-start(), calls=%async_computation.70 | async-start | bytes 1179648 | tf_op jit(solution)/shard_map/reduce_scatter | solution.py:20
  348.4 32.8 %reduce-scatter.83.cloned.1.call-start = ((), (), s32[]{:S(2)}) async-start(), calls=%async_computation.71 | async-start | bytes 1179648 | tf_op jit(solution)/shard_map/reduce_scatter | solution.py:20
  368.9 32.8 %reduce-scatter.85.cloned.1.call-start = ((), (), s32[]{:S(2)}) async-start(), calls=%async_computation.72 | async-start | bytes 1179648 | tf_op jit(solution)/shard_map/reduce_scatter | solution.py:20
  389.4 32.8 %reduce-scatter.87.cloned.1.call-start = ((), (), s32[]{:S(2)}) async-start(), calls=%async_computation.73 | async-start | bytes 1179648 | tf_op jit(solution)/shard_map/reduce_scatter | solution.py:20
  410.0 32.8 %reduce-scatter.89.cloned.1.call-start = ((), (), s32[]{:S(2)}) async-start(), calls=%async_computation.74 | async-start | bytes 1179648 | tf_op jit(solution)/shard_map/reduce_scatter | solution.py:20
  430.5 33.2 %reduce-scatter.91.cloned.1.call-start = ((), (), s32[]{:S(2)}) async-start(), calls=%async_computation.75 | async-start | bytes 1179648 | tf_op jit(solution)/shard_map/reduce_scatter | solution.py:20
  451.4 32.8 %reduce-scatter.93.cloned.1.call-start = ((), (), s32[]{:S(2)}) async-start(), calls=%async_computation.76 | async-start | bytes 1179648 | tf_op jit(solution)/shard_map/reduce_scatter | solution.py:20
  471.9 32.8 %reduce-scatter.95.cloned.1.call-start = ((), (), s32[]{:S(2)}) async-start(), calls=%async_computation.77 | async-start | bytes 1179648 | tf_op jit(solution)/shard_map/reduce_scatter | solution.py:20
  492.4 32.8 %reduce-scatter.97.cloned.1.call-start = ((), (), s32[]{:S(2)}) async-start(), calls=%async_computation.78 | async-start | bytes 1179648 | tf_op jit(solution)/shard_map/reduce_scatter | solution.py:20
  512.9 32.8 %reduce-scatter.99.cloned.1.call-start = ((), (), s32[]{:S(2)}) async-start(), calls=%async_computation.79 | async-start | bytes 1179648 | tf_op jit(solution)/shard_map/reduce_scatter | solution.py:20
  533.4 32.8 %reduce-scatter.101.cloned.1.call-start = ((), (), s32[]{:S(2)}) async-start(), calls=%async_computation.80 | async-start | bytes 1179648 | tf_op jit(solution)/shard_map/reduce_scatter | solution.py:20
  553.9 32.8 %reduce-scatter.103.cloned.1.call-start = ((), (), s32[]{:S(2)}) async-start(), calls=%async_computation.81 | async-start | bytes 1179648 | tf_op jit(solution)/shard_map/reduce_scatter | solution.py:20
  574.5 33.0 %reduce-scatter.105.cloned.1.call-start = ((), (), s32[]{:S(2)}) async-start(), calls=%async_computation.82 | async-start | bytes 1179648 | tf_op jit(solution)/shard_map/reduce_scatter | solution.py:20
  595.1 32.8 %reduce-scatter.107.cloned.1.call-start = ((), (), s32[]{:S(2)}) async-start(), calls=%async_computation.83 | async-start | bytes 1179648 | tf_op jit(solution)/shard_map/reduce_scatter | solution.py:20
  615.7 32.8 %reduce-scatter.109.cloned.1.call-start = ((), (), s32[]{:S(2)}) async-start(), calls=%async_computation.84 | async-start | bytes 1179648 | tf_op jit(solution)/shard_map/reduce_scatter | solution.py:20
  636.2 32.8 %reduce-scatter.111.cloned.1.call-start = ((), (), s32[]{:S(2)}) async-start(), calls=%async_computation.85 | async-start | bytes 1179648 | tf_op jit(solution)/shard_map/reduce_scatter | solution.py:20
  656.7 32.8 %reduce-scatter.113.cloned.1.call-start = ((), (), s32[]{:S(2)}) async-start(), calls=%async_computation.86 | async-start | bytes 1179648 | tf_op jit(solution)/shard_map/reduce_scatter | solution.py:20
  677.2 32.8 %reduce-scatter.115.cloned.1.call-start = ((), (), s32[]{:S(2)}) async-start(), calls=%async_computation.87 | async-start | bytes 1179648 | tf_op jit(solution)/shard_map/reduce_scatter | solution.py:20
  697.7 32.8 %reduce-scatter.117.cloned.1.call-start = ((), (), s32[]{:S(2)}) async-start(), calls=%async_computation.88 | async-start | bytes 1179648 | tf_op jit(solution)/shard_map/reduce_scatter | solution.py:20
  718.2 33.0 %reduce-scatter.119.cloned.1.call-start = ((), (), s32[]{:S(2)}) async-start(), calls=%async_computation.89 | async-start | bytes 1179648 | tf_op jit(solution)/shard_map/reduce_scatter | solution.py:20
  739.0 32.8 %reduce-scatter.121.cloned.1.call-start = ((), (), s32[]{:S(2)}) async-start(), calls=%async_computation.90 | async-start | bytes 1179648 | tf_op jit(solution)/shard_map/reduce_scatter | solution.py:20
  759.5 32.8 %reduce-scatter.123.cloned.1.call-start = ((), (), s32[]{:S(2)}) async-start(), calls=%async_computation.91 | async-start | bytes 1179648 | tf_op jit(solution)/shard_map/reduce_scatter | solution.py:20
  780.0 32.8 %reduce-scatter.125.cloned.1.call-start = ((), (), s32[]{:S(2)}) async-start(), calls=%async_computation.92 | async-start | bytes 1179648 | tf_op jit(solution)/shard_map/reduce_scatter | solution.py:20
  800.5 32.8 %reduce-scatter.127.cloned.1.call-start = ((), (), s32[]{:S(2)}) async-start(), calls=%async_computation.93 | async-start | bytes 1179648 | tf_op jit(solution)/shard_map/reduce_scatter | solution.py:20
  821.0 32.8 %reduce-scatter.129.cloned.1.call-start = ((), (), s32[]{:S(2)}) async-start(), calls=%async_computation.94 | async-start | bytes 1179648 | tf_op jit(solution)/shard_map/reduce_scatter | solution.py:20
  841.5 32.8 %reduce-scatter.131.cloned.1.call-start = ((), (), s32[]{:S(2)}) async-start(), calls=%async_computation.95 | async-start | bytes 1179648 | tf_op jit(solution)/shard_map/reduce_scatter | solution.py:20
  862.0 33.2 %reduce-scatter.133.cloned.1.call-start = ((), (), s32[]{:S(2)}) async-start(), calls=%async_computation.96 | async-start | bytes 1179648 | tf_op jit(solution)/shard_map/reduce_scatter | solution.py:20
  882.9 32.8 %reduce-scatter.135.cloned.1.call-start = ((), (), s32[]{:S(2)}) async-start(), calls=%async_computation.97 | async-start | bytes 1179648 | tf_op jit(solution)/shard_map/reduce_scatter | solution.py:20
  903.5 32.8 %reduce-scatter.137.cloned.1.call-start = ((), (), s32[]{:S(2)}) async-start(), calls=%async_computation.98 | async-start | bytes 1179648 | tf_op jit(solution)/shard_map/reduce_scatter | solution.py:20
  924.0 32.8 %reduce-scatter.139.cloned.1.call-start = ((), (), s32[]{:S(2)}) async-start(), calls=%async_computation.99 | async-start | bytes 1179648 | tf_op jit(solution)/shard_map/reduce_scatter | solution.py:20
  944.5 108.1 %reduce-scatter.141.cloned.1.call-start = ((), (), s32[]{:S(2)}) async-start(), calls=%async_computation.100 | async-start | bytes 1179648 | tf_op jit(solution)/shard_map/reduce_scatter | solution.py:20
  965.9 119.2 %reduce-scatter.143.cloned.1.call-start = ((), (), s32[]{:S(2)}) async-start(), calls=%async_computation.101 | async-start | bytes 1179648 | tf_op jit(solution)/shard_map/reduce_scatter | solution.py:20
  1062.3 293.8 %all-reduce.4.cloned.1.call-start = ((), (), s32[]{:S(2)}) async-start(), calls=%async_computation.102 | async-start | bytes 49840128 | tf_op jit(solution)/shard_map/psum | solution.py:71
  (98 other events, 723.7 us)
Sparse Core Ops, SparseCore 0:
  18.5 13.4 reduce-scatter.48
  40.4 12.1 reduce-scatter.50
  60.9 12.1 reduce-scatter.52
  81.5 12.1 reduce-scatter.54
  102.0 12.1 reduce-scatter.56
  122.5 12.1 reduce-scatter.58
  143.0 12.1 reduce-scatter.60
  163.7 12.1 reduce-scatter.62
  184.2 12.1 reduce-scatter.64
  204.7 12.1 reduce-scatter.66
  225.2 12.1 reduce-scatter.68
  245.8 12.1 reduce-scatter.70
  266.3 12.1 reduce-scatter.72
  286.8 12.1 reduce-scatter.74
  307.5 12.1 reduce-scatter.76
  328.0 12.1 reduce-scatter.78
  348.5 12.1 reduce-scatter.80
  369.1 12.1 reduce-scatter.82
  389.6 12.1 reduce-scatter.84
  410.1 12.1 reduce-scatter.86
  430.6 12.1 reduce-scatter.88
  451.5 12.1 reduce-scatter.90
  472.0 12.1 reduce-scatter.92
  492.5 12.1 reduce-scatter.94
  513.0 12.1 reduce-scatter.96
  533.6 12.1 reduce-scatter.98
  554.1 12.1 reduce-scatter.100
  574.6 12.1 reduce-scatter.102
  595.3 12.1 reduce-scatter.104
  615.8 12.1 reduce-scatter.106
  636.3 12.1 reduce-scatter.108
  656.8 12.1 reduce-scatter.110
  677.3 12.1 reduce-scatter.112
  697.8 12.1 reduce-scatter.114
  718.3 12.1 reduce-scatter.116
  739.1 12.1 reduce-scatter.118
  759.6 12.1 reduce-scatter.120
  780.1 12.1 reduce-scatter.122
  800.6 12.1 reduce-scatter.124
  821.1 12.1 reduce-scatter.126
  841.6 12.1 reduce-scatter.128
  862.1 12.1 reduce-scatter.130
  883.0 12.1 reduce-scatter.132
  903.6 12.1 reduce-scatter.134
  924.1 12.1 reduce-scatter.136
  944.6 12.1 reduce-scatter.138
  966.0 12.1 reduce-scatter.140
  1131.1 224.9 all-reduce.3
  (1 shorter events, 7.1 us)
where the time goes:
time: 1390 us; the launch traced here: 1380 us
  waiting for transfers between devices  698 us (50%)
  matrix products  308 us (22%)
  blocking collectives  259 us (19%)
  other arithmetic  65.6 us (5%)
  local copies, waits for them, and re-layouts  25.4 us (2%)
  between operations  22.1 us (2%)
    reduce_scatter x48, waiting for transfers between devices, teacher_layer(): lax.psum_scatter(partial_out, 'model', scatter_dimension=1, tiled=True)  542 us
    dot_general x48, matrix products, teacher_layer(): jnp.einsum('bsf,fd->bsd', activated, w_out, preferred_element_type=jnp.fl...  232 us
    psum x1, waiting for transfers between devices, student_grads(): return lax.psum(local_sums, ALL_AXES)  155 us
    all_gather x48, blocking collectives, teacher_layer(): gathered = lax.all_gather(normed, 'model', axis=1, tiled=True)  103 us
    psum x1, blocking collectives, student_grads(): count = lax.psum(jnp.sum(lengths).astype(jnp.float32), ALL_AXES)  66.5 us
    psum x1, blocking collectives, student_grads(): return lax.psum(local_sums, ALL_AXES)  64.1 us
    reduce_sum x49, other arithmetic, rms_gain(): jnp.mean(wide * wide, axis=-1, keepdims=True) + RMS_EPS  54.4 us
  transfers between devices with their start and end apart: 49, of which 47 were waited for; matrix products, arithmetic and copies ran while one was open for 3% of the time, Pallas kernels for 0%

commit v1 on v0

v1 whole, which is shorter than its diff:
```python
import functools

import jax
import jax.numpy as jnp
from jax import lax
from jax.experimental import pallas as pl
from jax.experimental.pallas import tpu as pltpu
from jax.sharding import PartitionSpec as P

RMS_EPS = 1e-6
ALL_AXES = ('data', 'model')
MESH = pl.DeviceIdType.MESH
GELU_C = 0.7978845608028654
GELU_A = 0.044715
F32 = jnp.float32
BF16 = jnp.bfloat16


def gelu(x):
    return x * (0.5 * (1.0 + jnp.tanh(GELU_C * (x + GELU_A * (x * x * x)))))


def gelu_grad(x):
    sq = x * x
    t = jnp.tanh(GELU_C * (x + GELU_A * (sq * x)))
    return 0.5 * (1.0 + t) + (0.5 * x) * (1.0 - t * t) * (GELU_C * (1.0 + (3.0 * GELU_A) * sq))


def inv_rms(wide):
    return lax.rsqrt(jnp.mean(wide * wide, axis=-1, keepdims=True) + RMS_EPS)


def teacher_kernel(layers, per_group, x_ref, gain_ref, w1_hbm, w2_hbm, feat_ref,
                   xbuf, hbuf, ubuf, part, recv, w1buf, w2buf,
                   x_send, x_recv, w_sem, p_send, p_recv):
    core = lax.axis_index('model')
    peer = {'model': 1 - core}
    seqs, pos, width = hbuf.shape
    hidden = ubuf.shape[1]
    n_out = part.shape[1]
    out_w = part.shape[3]
    slots = w1buf.shape[0]
    half = hidden // 3

    def fetch(layer, slot):
        return (pltpu.make_async_copy(w1_hbm.at[layer], w1buf.at[slot], w_sem.at[slot, 0]),
                pltpu.make_async_copy(w2_hbm.at[layer], w2buf.at[slot], w_sem.at[slot, 1]))

    for layer in range(slots - 1):
        for copy in fetch(layer, layer):
            copy.start()

    barrier = pltpu.get_barrier_semaphore()
    pl.semaphore_signal(barrier, inc=1, device_id=peer, device_id_type=MESH)
    pl.semaphore_wait(barrier, 1)

    x_copy = pltpu.make_async_remote_copy(x_ref, xbuf.at[core], x_send, x_recv, device_id=peer, device_id_type=MESH)
    x_copy.start()
    xbuf[core] = x_ref[...]
    x_copy.wait()
    for seq in range(seqs):
        for c in range(2):
            hbuf[seq, c * (pos // 2):(c + 1) * (pos // 2), :] = xbuf[c, seq]

    def exchange(seq, slot, c):
        return pltpu.make_async_remote_copy(
            part.at[seq, c], recv.at[slot, seq, c], p_send.at[seq, c], p_recv.at[slot, seq, c],
            device_id=peer, device_id_type=MESH)

    def absorb(seq, slot):
        for c in range(n_out):
            exchange(seq, slot, c).wait()
            cols = slice(c * out_w, (c + 1) * out_w)
            update = part[seq, c] + recv[slot, seq, c]
            hbuf[seq, :, cols] = (hbuf[seq, :, cols].astype(F32) + update).astype(BF16)

    def block(layer, _):
        slot = lax.rem(layer, slots)

        @pl.when(layer + (slots - 1) < layers)
        def _():
            for copy in fetch(layer + (slots - 1), lax.rem(layer + (slots - 1), slots)):
                copy.start()

        fetched = fetch(layer, slot)
        for seq in range(seqs):
            @pl.when(layer > 0)
            def _():
                absorb(seq, lax.rem(layer + 1, 2))
            if seq == 0:
                fetched[0].wait()
            wide = hbuf[seq].astype(F32)
            normed = (wide * inv_rms(wide) * gain_ref[layer]).astype(BF16)
            for c in range(3):
                cols = slice(c * half, (c + 1) * half)
                pre = jnp.dot(normed, w1buf[slot, :, cols], preferred_element_type=F32)
                ubuf[:, cols] = gelu(pre).astype(BF16)
            if seq == 0:
                fetched[1].wait()
            act = ubuf[...]
            for c in range(n_out):
                part[seq, c] = jnp.dot(act, w2buf[slot, :, c * out_w:(c + 1) * out_w], preferred_element_type=F32)
                exchange(seq, lax.rem(layer, 2), c).start()

        @pl.when((layer > 0) & (lax.rem(layer, per_group) == 0))
        def _():
            feat_ref[lax.div(layer, per_group) - 1] = hbuf[core]
        return 0

    lax.fori_loop(0, layers, block, 0)
    for seq in range(seqs):
        absorb(seq, (layers - 1) % 2)
    feat_ref[layers // per_group - 1] = hbuf[core]


def teacher(x_t, t_w1, t_w2, t_gain, n_feat):
    layers, width, hidden = t_w1.shape
    seqs, half_pos, _ = x_t.shape
    pos = 2 * half_pos
    slots, n_out = 3, 3
    out_w = width // n_out
    vmem = pl.BlockSpec(memory_space=pltpu.VMEM)
    hbm = pl.BlockSpec(memory_space=pl.ANY)
    return pl.pallas_call(
        functools.partial(teacher_kernel, layers, layers // n_feat),
        out_shape=jax.ShapeDtypeStruct((n_feat, pos, width), BF16),
        in_specs=[vmem, vmem, hbm, hbm],
        out_specs=vmem,
        scratch_shapes=[
            pltpu.VMEM((2, seqs, half_pos, width), BF16),
            pltpu.VMEM((seqs, pos, width), BF16),
            pltpu.VMEM((pos, hidden), BF16),
            pltpu.VMEM((seqs, n_out, pos, out_w), F32),
            pltpu.VMEM((2, seqs, n_out, pos, out_w), F32),
            pltpu.VMEM((slots, width, hidden), BF16),
            pltpu.VMEM((slots, hidden, width), BF16),
            pltpu.SemaphoreType.DMA,
            pltpu.SemaphoreType.DMA,
            pltpu.SemaphoreType.DMA((slots, 2)),
            pltpu.SemaphoreType.DMA((seqs, n_out)),
            pltpu.SemaphoreType.DMA((2, seqs, n_out)),
        ],
        compiler_params=pltpu.CompilerParams(collective_id=0, has_side_effects=True,
                                             vmem_limit_bytes=40 * 1024 * 1024),
        cost_estimate=pl.CostEstimate(flops=4 * seqs * pos * width * hidden * layers,
                                      bytes_accessed=4 * layers * width * hidden, transcendentals=0),
        name='teacher',
    )(x_t, t_gain.reshape(layers, 1, width), t_w1, t_w2)


def dot_tn(a, b):
    return lax.dot_general(a, b, (((0,), (0,)), ((), ())), preferred_element_type=F32)


def dot_nt(a, b):
    return lax.dot_general(a, b, (((1,), (1,)), ((), ())), preferred_element_type=F32)


def rms_back(dy, x, gain):
    r = inv_rms(x)
    xr = x * r
    gdy = dy * gain
    dx = r * (gdy - xr * jnp.mean(gdy * xr, axis=-1, keepdims=True))
    return dx, jnp.sum(dy * xr, axis=0, keepdims=True)


def student_kernel(len_ref, x_ref, feat_ref, w1_ref, w2_ref, g1_ref, g2_ref, proj_ref,
                   gw1_ref, gw2_ref, gg1_ref, gg2_ref, gproj_ref, sq_ref,
                   s_in, s_out, normed_s, pre_s, act_s, dproj_s):
    layers = w1_ref.shape[0]
    pos = x_ref.shape[1]
    valid = (lax.broadcasted_iota(jnp.int32, (pos, 1), 0) < len_ref[0]).astype(F32)

    def forward(layer, carry):
        state, sq = carry
        s_in[layer] = state
        normed = (state * inv_rms(state) * g1_ref[layer]).astype(BF16)
        normed_s[layer] = normed
        pre = jnp.dot(normed, w1_ref[layer], preferred_element_type=F32)
        pre_s[layer] = pre
        act = gelu(pre).astype(BF16)
        act_s[layer] = act
        state = (state + jnp.dot(act, w2_ref[layer], preferred_element_type=F32)).astype(BF16).astype(F32)
        normed_out = (state * inv_rms(state) * g2_ref[layer]).astype(BF16)
        err = (jnp.dot(normed_out, proj_ref[layer], preferred_element_type=F32) - feat_ref[layer].astype(F32)) * valid
        sq = sq + jnp.sum(jnp.sum(err * err, axis=0, keepdims=True), axis=1, keepdims=True)
        d_err = err.astype(BF16)
        gproj_ref[layer] = dot_tn(normed_out, d_err)
        d_out = dot_nt(d_err, proj_ref[layer])
        dx, dg = rms_back(d_out, state, g2_ref[layer])
        dproj_s[layer] = dx
        gg2_ref[layer] = dg
        return state, sq

    _, sq = lax.fori_loop(0, layers, forward, (x_ref[0].astype(F32), jnp.zeros((1, 1), F32)))
    sq_ref[...] = sq

    def backward(step, d_state):
        layer = layers - 1 - step
        d_state = d_state + dproj_s[layer]
        d_update = d_state.astype(BF16)
        gw2_ref[layer] = dot_tn(act_s[layer], d_update)
        d_act = dot_nt(d_update, w2_ref[layer])
        d_pre = (d_act * gelu_grad(pre_s[layer])).astype(BF16)
        gw1_ref[layer] = dot_tn(normed_s[layer], d_pre)
        d_norm = dot_nt(d_pre, w1_ref[layer])
        dx, dg = rms_back(d_norm, s_in[layer], g1_ref[layer])
        gg1_ref[layer] = dg
        return d_state + dx

    lax.fori_loop(0, layers, backward, jnp.zeros(s_in.shape[1:], F32))


def student(x_s, lengths, feats, s_w1, s_w2, s_gain1, s_gain2, s_proj):
    layers, width, hidden = s_w1.shape
    t_width = s_proj.shape[2]
    pos = x_s.shape[1]
    vmem = pl.BlockSpec(memory_space=pltpu.VMEM)
    smem = pl.BlockSpec(memory_space=pltpu.SMEM)
    return pl.pallas_call(
        student_kernel,
        out_shape=(jax.ShapeDtypeStruct((layers, width, hidden), F32),
                   jax.ShapeDtypeStruct((layers, hidden, width), F32),
                   jax.ShapeDtypeStruct((layers, 1, width), F32),
                   jax.ShapeDtypeStruct((layers, 1, width), F32),
                   jax.ShapeDtypeStruct((layers, width, t_width), F32),
                   jax.ShapeDtypeStruct((1, 1), F32)),
        in_specs=[smem] + [vmem] * 7,
        out_specs=[vmem] * 6,
        scratch_shapes=[
            pltpu.VMEM((layers, pos, width), F32),
            pltpu.VMEM((1, 1), F32),
            pltpu.VMEM((layers, pos, width), BF16),
            pltpu.VMEM((layers, pos, hidden), F32),
            pltpu.VMEM((layers, pos, hidden), BF16),
            pltpu.VMEM((layers, pos, width), F32),
        ],
        compiler_params=pltpu.CompilerParams(vmem_limit_bytes=63 * 1024 * 1024),
        name='student',
    )(lengths, x_s, feats, s_w1, s_w2, s_gain1.reshape(layers, 1, width), s_gain2.reshape(layers, 1, width), s_proj)


def solution(mesh):
    def body(x_t, x_s, lengths, t_w1, t_w2, t_gain, s_w1, s_w2, s_gain1, s_gain2, s_proj):
        n_feat = s_w1.shape[0]
        feats = teacher(x_t, t_w1, t_w2, t_gain, n_feat)
        gw1, gw2, gg1, gg2, gproj, sq = student(x_s, lengths, feats, s_w1, s_w2, s_gain1, s_gain2, s_proj)
        tokens = jnp.sum(lengths).astype(F32)
        gw1, gw2, gproj, gg1, gg2, sq, tokens = lax.psum((gw1, gw2, gproj, gg1, gg2, sq, tokens), ALL_AXES)
        inv = 1.0 / (n_feat * x_t.shape[2] * tokens)
        two = 2.0 * inv
        shape = s_gain1.shape
        return (sq[0, 0] * inv, gw1 * two, gw2 * two, gg1.reshape(shape) * two, gg2.reshape(shape) * two, gproj * two)

    in_specs = (P('data', 'model', None), P(ALL_AXES, None, None), P(ALL_AXES),
                P(None, None, 'model'), P(None, 'model', None), P(), P(), P(), P(), P(), P())
    out_specs = (P(), P(), P(), P(), P(), P())
    return jax.shard_map(body, mesh=mesh, in_specs=in_specs, out_specs=out_specs, check_vma=False)
```

time: 1390 us -> 498 us (0.36)
  waiting for transfers between devices: 698 us -> 161 us
  matrix products: 308 us -> 0 us
  Pallas kernels: 0 us -> 197 us
  blocking collectives: 259 us -> 70.6 us
  other arithmetic: 65.6 us -> 23 us
    reduce_scatter x48 -> x0, waiting for transfers between devices: 542 us -> none  [teacher_layer(): lax.psum_scatter(partial_out, 'model', scatter_dimension=1, tiled=True)]
    dot_general x102 -> x0, matrix products: 308 us -> none  [the longest x48 232 us: teacher_layer(): jnp.einsum('bsf,fd->bsd', activated, w_out, preferred_element_type=jnp.fl...]
    pallas_call x0 -> x2, Pallas kernels: none -> 197 us  [the longest x1 167 us: teacher(): pl.pallas_call(functools.partial(teacher_kernel, layers, layers // n_feat...]
    all_gather x48 -> x0, blocking collectives: 103 us -> none  [teacher_layer(): gathered = lax.all_gather(normed, 'model', axis=1, tiled=True)]
    psum x2 -> x1, blocking collectives: 131 us -> 70.6 us  [body(): lax.psum((gw1, gw2, gproj, gg1, gg2, sq, tokens), ALL_AXES)]
    reduce_sum x49 -> x0, other arithmetic: 54.4 us -> none  [rms_gain(): jnp.mean(wide * wide, axis=-1, keepdims=True) + RMS_EPS]
    all_to_all x6 -> x0, blocking collectives: 25.2 us -> none  [body(): features.append(lax.all_to_all(hidden, 'model', 0, 1, tiled=True))]
    mul x0 -> x4, other arithmetic: none -> 23 us  [the longest x1 9.34 us: body(): gw2 * two]
  transfers between devices with their start and end apart: 49 -> 1, of which waited for: 47 -> 1; matrix products, arithmetic and copies ran while one was open for 3% -> 0% of each run, Pallas kernels for 0% -> 0%
where the time goes in v1:
time: 498 us; the launch traced here: 497 us
  Pallas kernels  197 us (40%)
  waiting for transfers between devices  161 us (32%)
  blocking collectives  70.6 us (14%)
  local copies, waits for them, and re-layouts  29.1 us (6%)
  other arithmetic  23 us (5%)
  between operations  17.2 us (3%)
    pallas_call x1, Pallas kernels, teacher(): pl.pallas_call(functools.partial(teacher_kernel, layers, layers // n_feat...  167 us
    psum x1, waiting for transfers between devices, body(): lax.psum((gw1, gw2, gproj, gg1, gg2, sq, tokens), ALL_AXES)  161 us
    psum x1, blocking collectives, body(): lax.psum((gw1, gw2, gproj, gg1, gg2, sq, tokens), ALL_AXES)  70.6 us
    pallas_call x1, Pallas kernels, student(): pl.pallas_call(student_kernel, out_shape=(jax.ShapeDtypeStruct((layers, w...  30.1 us
    unnamed x13, local copies, waits for them, and re-layouts  25.5 us
  transfers between devices with their start and end apart: 1, of which 1 were waited for; matrix products, arithmetic and copies ran while one was open for 0% of the time, Pallas kernels for 0%

profile of v1, /device:TPU:1, one launch (start us, length us, event | category | flops | bytes accessed | tf_op | source)
XLA Modules:
  0.0 497.5 jit_solution(12953694256531088602)
XLA Ops:
  7.2 0.0 copy-start.1
  7.2 0.0 all-reduce.4.cloned.1.call-start
  7.9 1.3 reshape.30.g1_ref
  9.2 1.3 reshape.31.g2_ref
  10.5 1.6 copy.17.x_ref
  12.2 1.0 reshape.29.gain_ref
  13.2 8.3 %copy.18.w2_ref = bf16[6,1248,312]{2,1,0:T(8,128)(2,1)} copy(bf16[6,1248,312]{1,2,0:T(8,128)(2,1)} %param.18) | data formatting | bytes 9345024 | tf_op args[7]
  21.5 0.0 copy-done.1
  21.5 166.7 %teacher.1.feat_ref = bf16[6,128,768]{2,1,0:T(8,128)(2,1)S(1)} custom-call(bf16[2,64,768]{2,1,0:T(8,128)(2,1)S(1)} %copy-done.1, f32[48,1,768]{2,1,0:T(1,128)S(1)} %reshape.29.gain_ref, bf16[48,768,1536]{2,1,0:T(8,128)(2,1)} %w1_hbm.1, bf16[48,1536,768]{2,1,0:T(8,128)(2,1)} %w2_hbm.1), custom_call_target="tpu_custom_call" | custom-call | flops 57982058496 | bytes 226492416 | tf_op jit(solution)/shard_map/teacher/pallas_call | solution.py:124
  188.2 0.0 copy-start
  188.2 1.0 copy-done
  189.2 30.1 %student.1 = (f32[6,312,1248]{2,1,0:T(8,128)}, f32[6,1248,312]{2,1,0:T(8,128)}, f32[6,1,312]{2,1,0:T(1,128)}, f32[6,1,312]{2,1,0:T(1,128)}, f32[6,312,768]{2,1,0:T(8,128)}, /*index=5*/f32[1,1]{1,0:T(1,128)}) custom-call(s32[1]{0:T(128)S(6)} %copy.29.len_ref, bf16[1,128,312]{2,1,0:T(8,128)(2,1)} %copy.17.x_ref, bf16[6,128,768]{2,1,0:T(8,128)(2,1)} %copy-done, ...), custom_call_target="tpu_custom_call" | custom-call | tf_op jit(solution)/shard_map/student/pallas_call | solution.py:220
  219.3 0.0 copy-start.2
  219.3 0.0 copy-start.3
  219.3 0.0 all-reduce.4.cloned.1.call-update
  219.3 0.7 copy-done.2
  220.0 0.0 copy-done.3
  220.0 70.6 %all-reduce = (f32[]{:T(128)}, f32[]{:T(128)}, f32[6,1,312]{2,1,0:T(1,128)S(1)}, f32[6,1,312]{2,1,0:T(1,128)S(1)}) all-reduce(f32[]{:T(128)} %bitcast, f32[]{:T(128)} %bitcast.1, f32[6,1,312]{2,1,0:T(1,128)S(1)} %copy-done.2, f32[6,1,312]{2,1,0:T(1,128)S(1)} %copy-done.3), channel_id=1, replica_groups=mesh['data'=64,'model'=2] {'data','model'}, use_global_device_ids=true, to_apply=%region_0.0 | all-reduce | flops 3746 | bytes 29968 | tf_op jit(solution)/shard_map/psum | solution.py:249
  292.0 0.6 copy.24
  292.6 0.6 copy.25
  293.2 160.7 %all-reduce.4.cloned.1.call-done = (f32[6,312,1248]{2,1,0:T(8,128)}, f32[6,1248,312]{2,1,0:T(8,128)}, f32[6,312,768]{2,1,0:T(8,128)}) async-done(((f32[6,312,1248]{2,1,0:T(8,128)}, f32[6,1248,312]{2,1,0:T(8,128)}, f32[6,312,768]{2,1,0:T(8,128)}), (f32[6,312,1248]{2,1,0:T(8,128)}, f32[6,1248,312]{2,1,0:T(8,128)}, f32[6,312,768]{2,1,0:T(8,128)})) %all-reduce.4.cloned.1.call-update) | async-done | bytes 24440848 | tf_op jit(solution)/shard_map/psum | solution.py:249
  453.9 5.5 %broadcast_multiply_fusion.2 = f32[6,312,768]{2,1,0:T(8,128)} fusion(f32[6,312,768]{2,1,0:T(8,128)} %get-tuple-element.30, f32[]{:T(128)S(6)} %mul_shard_map.7), kind=kLoop, calls=%fused_computation.2 | loop fusion | flops 1437696 | bytes 11501572 | tf_op jit(solution)/shard_map/mul | solution.py:253
  459.4 9.3 %broadcast_multiply_fusion = f32[6,1248,312]{2,1,0:T(8,128)} fusion(f32[6,1248,312]{2,1,0:T(8,128)} %get-tuple-element.29, f32[]{:T(128)S(6)} %mul_shard_map.7), kind=kLoop, calls=%fused_computation | loop fusion | flops 2336256 | bytes 18690052 | tf_op jit(solution)/shard_map/mul | solution.py:253
  468.7 12.6 %copy.19 = f32[6,1248,312]{1,2,0:T(8,128)} copy(f32[6,1248,312]{2,1,0:T(8,128)} %broadcast_multiply_fusion) | data formatting | bytes 18690048
  481.4 8.1 %broadcast_multiply_fusion.1 = f32[6,312,1248]{2,1,0:T(8,128)} fusion(f32[6,312,1248]{2,1,0:T(8,128)} %get-tuple-element.28, f32[]{:T(128)S(6)} %mul_shard_map.7), kind=kLoop, calls=%fused_computation.1 | loop fusion | flops 2336256 | bytes 18690052 | tf_op jit(solution)/shard_map/mul | solution.py:253
  (1 shorter events, 0.0 us)
Async XLA Ops:
  7.2 14.3 %copy-start.1 = (bf16[2,64,768]{2,1,0:T(8,128)(2,1)S(1)}, bf16[2,64,768]{2,1,0:T(8,128)(2,1)}, u32[]{:S(2)}) copy-start(bf16[2,64,768]{2,1,0:T(8,128)(2,1)} %x_ref.2) | copy-start | bytes 589828
  7.2 446.7 %all-reduce.4.cloned.1.call-start = ((), (), s32[]{:S(2)}) async-start(), calls=%async_computation | async-start | bytes 53673984 | tf_op jit(solution)/shard_map/psum | solution.py:249
  188.2 1.0 copy-start
  219.3 0.7 copy-start.2
  219.3 0.7 copy-start.3
Sparse Core Ops, SparseCore 0:
  219.5 234.3 all-reduce.3

commit v2 on v1

--- a/solution.py
+++ b/solution.py
@@ -90,7 +90,7 @@
             if seq == 0:
                 fetched[0].wait()
             wide = hbuf[seq].astype(F32)
-            normed = (wide * inv_rms(wide) * gain_ref[layer]).astype(BF16)
+            normed = (wide * inv_rms(wide) * gain_ref[pl.ds(layer, 1), :]).astype(BF16)
             for c in range(3):
                 cols = slice(c * half, (c + 1) * half)
                 pre = jnp.dot(normed, w1buf[slot, :, cols], preferred_element_type=F32)
@@ -145,7 +145,7 @@
         cost_estimate=pl.CostEstimate(flops=4 * seqs * pos * width * hidden * layers,
                                       bytes_accessed=4 * layers * width * hidden, transcendentals=0),
         name='teacher',
-    )(x_t, t_gain.reshape(layers, 1, width), t_w1, t_w2)
+    )(x_t, t_gain, t_w1, t_w2)
 
 
 def dot_tn(a, b):
@@ -164,93 +164,407 @@
     return dx, jnp.sum(dy * xr, axis=0, keepdims=True)
 
 
-def student_kernel(len_ref, x_ref, feat_ref, w1_ref, w2_ref, g1_ref, g2_ref, proj_ref,
-                   gw1_ref, gw2_ref, gg1_ref, gg2_ref, gproj_ref, sq_ref,
-                   s_in, s_out, normed_s, pre_s, act_s, dproj_s):
+TILES = 1024
+ROW_TILES = 39
+W2_AT, W1_AT, SMALL_AT = 234, 624, 1014
+SQ_TILE, COUNT_TILE = SMALL_AT + 6, SMALL_AT + 7
+PARTS = ((0, W2_AT), (W2_AT, W1_AT - W2_AT), (W1_AT, TILES - W1_AT))
+
+
+def store_tiles(ref, idx, start, value):
+    width = value.shape[1]
+    for ct in range(-(-width // 128)):
+        lanes = min(128, width - ct * 128)
+        piece = value[:, ct * 128:ct * 128 + lanes]
+        if lanes < 128:
+            piece = jnp.concatenate([piece, jnp.zeros((piece.shape[0], 128 - lanes), F32)], axis=1)
+        ref[idx, start + ct * ROW_TILES:start + (ct + 1) * ROW_TILES] = piece.reshape(ROW_TILES, 8, 128)
+
+
+def store_row(ref, idx, start, row):
+    width = row.shape[1]
+    for ct in range(-(-width // 128)):
+        lanes = min(128, width - ct * 128)
+        piece = row[:, ct * 128:ct * 128 + lanes]
+        if lanes < 128:
+            piece = jnp.concatenate([piece, jnp.zeros((1, 128 - lanes), F32)], axis=1)
+        ref[idx, start + ct] = jnp.broadcast_to(piece, (8, 128))
+
+
+def student_kernel(len_ref, x_ref, feat_ref, w1_ref, w2_ref, g1_ref, g2_ref, proj_ref, out_hbm,
+                   grad, recv, s_in, normed_s, pre_s, act_s, dproj_s, send_sem, recv_sem, out_sem):
+    core = lax.axis_index('model')
+    peer = {'model': 1 - core}
     layers = w1_ref.shape[0]
-    pos = x_ref.shape[1]
+    pairs = layers // 2
+    pos = x_ref.shape[2]
+    barrier = pltpu.get_barrier_semaphore()
+    pl.semaphore_signal(barrier, inc=1, device_id=peer, device_id_type=MESH)
+    pl.semaphore_wait(barrier, 1)
     valid = (lax.broadcasted_iota(jnp.int32, (pos, 1), 0) < len_ref[0]).astype(F32)
-
-    def forward(layer, carry):
-        state, sq = carry
+    tokens = jnp.broadcast_to(len_ref[0].astype(F32), (8, 128))
+
+    def send(pair, part):
+        start, size = PARTS[part]
+        return pltpu.make_async_remote_copy(
+            grad.at[pairs + pair, pl.ds(start, size)], recv.at[pair, pl.ds(start, size)],
+            send_sem.at[pair, part], recv_sem.at[pair, part], device_id=peer, device_id_type=MESH)
+
+    def place(layer):
+        pair = lax.div(layer, 2)
+        mine = lax.rem(layer, 2) == core
+        return pair, mine, jnp.where(mine, pair, pairs + pair)
+
+    def forward(layer, state):
+        pair, mine, idx = place(layer)
         s_in[layer] = state
-        normed = (state * inv_rms(state) * g1_ref[layer]).astype(BF16)
+        normed = (state * inv_rms(state) * g1_ref[pl.ds(layer, 1), :]).astype(BF16)
         normed_s[layer] = normed
         pre = jnp.dot(normed, w1_ref[layer], preferred_element_type=F32)
         pre_s[layer] = pre
         act = gelu(pre).astype(BF16)
         act_s[layer] = act
-        state = (state + jnp.dot(act, w2_ref[layer], preferred_element_type=F32)).astype(BF16).astype(F32)
-        normed_out = (state * inv_rms(state) * g2_ref[layer]).astype(BF16)
+        state = (state + dot_nt(act, w2_ref[layer])).astype(BF16).astype(F32)
+        normed_out = (state * inv_rms(state) * g2_ref[pl.ds(layer, 1), :]).astype(BF16)
         err = (jnp.dot(normed_out, proj_ref[layer], preferred_element_type=F32) - feat_ref[layer].astype(F32)) * valid
-        sq = sq + jnp.sum(jnp.sum(err * err, axis=0, keepdims=True), axis=1, keepdims=True)
+        sq = jnp.sum(jnp.sum(err * err, axis=0, keepdims=True), axis=1, keepdims=True)
         d_err = err.astype(BF16)
-        gproj_ref[layer] = dot_tn(normed_out, d_err)
-        d_out = dot_nt(d_err, proj_ref[layer])
-        dx, dg = rms_back(d_out, state, g2_ref[layer])
+        store_tiles(grad, idx, 0, dot_tn(normed_out, d_err))
+
+        @pl.when(jnp.logical_not(mine))
+        def _():
+            send(pair, 0).start()
+
+        dx, dg = rms_back(dot_nt(d_err, proj_ref[layer]), state, g2_ref[pl.ds(layer, 1), :])
         dproj_s[layer] = dx
-        gg2_ref[layer] = dg
-        return state, sq
-
-    _, sq = lax.fori_loop(0, layers, forward, (x_ref[0].astype(F32), jnp.zeros((1, 1), F32)))
-    sq_ref[...] = sq
+        store_row(grad, idx, SMALL_AT + 3, dg)
+        grad[idx, SQ_TILE] = jnp.broadcast_to(sq, (8, 128))
+        grad[idx, COUNT_TILE] = tokens
+        for spare in range(COUNT_TILE + 1, TILES):
+            grad[idx, spare] = jnp.zeros((8, 128), F32)
+        return state
+
+    lax.fori_loop(0, layers, forward, x_ref[0].astype(F32).T)
 
     def backward(step, d_state):
         layer = layers - 1 - step
+        pair, mine, idx = place(layer)
         d_state = d_state + dproj_s[layer]
         d_update = d_state.astype(BF16)
-        gw2_ref[layer] = dot_tn(act_s[layer], d_update)
-        d_act = dot_nt(d_update, w2_ref[layer])
+        store_tiles(grad, idx, W2_AT, dot_tn(d_update, act_s[layer]))
+
+        @pl.when(jnp.logical_not(mine))
+        def _():
+            send(pair, 1).start()
+
+        d_act = jnp.dot(d_update, w2_ref[layer], preferred_element_type=F32)
         d_pre = (d_act * gelu_grad(pre_s[layer])).astype(BF16)
-        gw1_ref[layer] = dot_tn(normed_s[layer], d_pre)
-        d_norm = dot_nt(d_pre, w1_ref[layer])
-        dx, dg = rms_back(d_norm, s_in[layer], g1_ref[layer])
-        gg1_ref[layer] = dg
+        dx, dg = rms_back(dot_nt(d_pre, w1_ref[layer]), s_in[layer], g1_ref[pl.ds(layer, 1), :])
+        store_row(grad, idx, SMALL_AT, dg)
+        store_tiles(grad, idx, W1_AT, dot_tn(normed_s[layer], d_pre))
+
+        @pl.when(jnp.logical_not(mine))
+        def _():
+            send(pair, 2).start()
+
         return d_state + dx
 
     lax.fori_loop(0, layers, backward, jnp.zeros(s_in.shape[1:], F32))
 
-
-def student(x_s, lengths, feats, s_w1, s_w2, s_gain1, s_gain2, s_proj):
+    def out_copy(pair):
+        return pltpu.make_async_copy(grad.at[pair], out_hbm.at[pair], out_sem.at[pair])
+
+    for pair in reversed(range(pairs)):
+        for part in range(3):
+            send(pair, part).wait_recv()
+            start, size = PARTS[part]
+            span = pl.ds(start, size)
+            grad[pair, span] = grad[pair, span] + recv[pair, span]
+        out_copy(pair).start()
+    for pair in range(pairs):
+        for part in range(3):
+            send(pair, part).wait_send()
+        out_copy(pair).wait()
+
+
+def student(x_s, lengths, feats, s_w1, s_w2t, s_gain1, s_gain2, s_proj):
     layers, width, hidden = s_w1.shape
-    t_width = s_proj.shape[2]
-    pos = x_s.shape[1]
+    pos = x_s.shape[2]
     vmem = pl.BlockSpec(memory_space=pltpu.VMEM)
-    smem = pl.BlockSpec(memory_space=pltpu.SMEM)
     return pl.pallas_call(
         student_kernel,
-        out_shape=(jax.ShapeDtypeStruct((layers, width, hidden), F32),
-                   jax.ShapeDtypeStruct((layers, hidden, width), F32),
-                   jax.ShapeDtypeStruct((layers, 1, width), F32),
-                   jax.ShapeDtypeStruct((layers, 1, width), F32),
-                   jax.ShapeDtypeStruct((layers, width, t_width), F32),
-                   jax.ShapeDtypeStruct((1, 1), F32)),
-        in_specs=[smem] + [vmem] * 7,
-        out_specs=[vmem] * 6,
+        out_shape=jax.ShapeDtypeStruct((layers // 2, TILES, 8, 128), F32),
+        in_specs=[pl.BlockSpec(memory_space=pltpu.SMEM)] + [vmem] * 7,
+        out_specs=pl.BlockSpec(memory_space=pl.ANY),
         scratch_shapes=[
+            pltpu.VMEM((layers, TILES, 8, 128), F32),
+            pltpu.VMEM((layers // 2, TILES, 8, 128), F32),
             pltpu.VMEM((layers, pos, width), F32),
-            pltpu.VMEM((1, 1), F32),
             pltpu.VMEM((layers, pos, width), BF16),
             pltpu.VMEM((layers, pos, hidden), F32),
             pltpu.VMEM((layers, pos, hidden), BF16),
             pltpu.VMEM((layers, pos, width), F32),
+            pltpu.SemaphoreType.DMA((layers // 2, 3)),
+            pltpu.SemaphoreType.DMA((layers // 2, 3)),
+            pltpu.SemaphoreType.DMA((layers // 2,)),
         ],
-        compiler_params=pltpu.CompilerParams(vmem_limit_bytes=63 * 1024 * 1024),
+        compiler_params=pltpu.CompilerParams(collective_id=1, has_side_effects=True,
+                                             vmem_limit_bytes=67_043_328),
         name='student',
-    )(lengths, x_s, feats, s_w1, s_w2, s_gain1.reshape(layers, 1, width), s_gain2.reshape(layers, 1, width), s_proj)
+    )(lengths, x_s, feats, s_w1, s_w2t, s_gain1, s_gain2, s_proj)
+
+
+def reduce_kernel(side, g_hbm, out_hbm, data, full, near, far,
+                  load_sem, rs_send, rs_recv, ag_send, ag_recv, own_sem, d2d_send, d2d_recv):
+    core = lax.axis_index('model')
+    chip = lax.axis_index('data')
+    peer = {'model': 1 - core}
+    colors = data.shape[0]
+    coord = [lax.rem(chip, side), lax.rem(lax.div(chip, side), side), lax.div(chip, side * side)]
+
+    def shifted(axis, by):
+        moved = list(coord)
+        moved[axis] = lax.rem(coord[axis] + by, side)
+        return {'data': (moved[2] * side + moved[1]) * side + moved[0]}
+
+    def load(c, a):
+        span = pl.ds(a * 256, 256)
+        return pltpu.make_async_copy(g_hbm.at[c, span], data.at[c, span], load_sem.at[c, a])
+
+    for a in range(4):
+        for c in range(colors):
+            load(c, a).start()
+
+    barrier = pltpu.get_barrier_semaphore()
+    pl.semaphore_signal(barrier, inc=1, device_id=peer, device_id_type=MESH)
+    for axis in range(3):
+        for by in (1, side - 1):
+            pl.semaphore_signal(barrier, inc=1, device_id=shifted(axis, by), device_id_type=MESH)
+    pl.semaphore_wait(barrier, 7)
+
+    for a in range(4):
+        for c in range(colors):
+            load(c, a).wait()
+
+    plus = [shifted(axis, 1) for axis in range(3)]
+    minus = [shifted(axis, side - 1) for axis in range(3)]
+    sent = []
+    base = [0] * colors
+    bases = []
+    near_at, far_at = 0, 0
+    size = 256
+
+    for phase in range(3):
+        half = size // 2
+        bases.append(list(base))
+
+        def chunk(c, by):
+            axis = (c + phase) % 3
+            return base[c] + lax.rem(coord[axis] + by, side) * size
+
+        def push(c, kind, src, dst, upward):
+            axis = (c + phase) % 3
+            copy = pltpu.make_async_remote_copy(
+                src, dst, rs_send.at[c, phase, kind], rs_recv.at[c, phase, kind],
+                device_id=plus[axis] if upward else minus[axis], device_id_type=MESH)
+            copy.start()
+            sent.append(copy)
+            return copy
+
+        first, early, late = {}, {}, {}
+        for c in range(colors):
+            opp, nxt, prv = chunk(c, 2), chunk(c, 1), chunk(c, 3)
+            first[c] = (
+                push(c, 0, data.at[c, pl.ds(opp, half)], near.at[c, 0, pl.ds(near_at, half)], True),
+                push(c, 1, data.at[c, pl.ds(opp + half, half)], near.at[c, 1, pl.ds(near_at, half)], False))
+            early[c] = (
+                push(c, 2, data.at[c, pl.ds(nxt + half, half)], far.at[c, 0, pl.ds(far_at + half, half)], True),
+                push(c, 3, data.at[c, pl.ds(prv, half)], far.at[c, 1, pl.ds(far_at, half)], False))
+        for c in range(colors):
+            nxt, prv = chunk(c, 1), chunk(c, 3)
+            first[c][0].wait_recv()
+            span = pl.ds(nxt, half)
+            data[c, span] = data[c, span] + near[c, 0, pl.ds(near_at, half)]
+            up = push(c, 4, data.at[c, span], far.at[c, 0, pl.ds(far_at, half)], True)
+            first[c][1].wait_recv()
+            span = pl.ds(prv + half, half)
+            data[c, span] = data[c, span] + near[c, 1, pl.ds(near_at, half)]
+            down = push(c, 5, data.at[c, span], far.at[c, 1, pl.ds(far_at + half, half)], False)
+            late[c] = (up, down)
+        for c in range(colors):
+            for copy in early[c] + late[c]:
+                copy.wait_recv()
+            mine = pl.ds(chunk(c, 0), size)
+            both = far[c, 0, pl.ds(far_at, size)] + far[c, 1, pl.ds(far_at, size)]
+            if phase < 2:
+                data[c, mine] = data[c, mine] + both
+            else:
+                full[c, mine] = data[c, mine] + both
+        base = [chunk(c, 0) for c in range(colors)]
+        near_at, far_at, size = near_at + half, far_at + size, half // 2
+
+    emitted = []
+
+    def emit(c, slot, start, count):
+        layer = 2 * c + core
+        span = pl.ds(start, count)
+        own = pltpu.make_async_copy(full.at[c, span], out_hbm.at[layer, span], own_sem.at[c, slot])
+        own.start()
+        across = pltpu.make_async_remote_copy(
+            full.at[c, span], out_hbm.at[layer, span], d2d_send.at[c, slot], d2d_recv.at[c, slot],
+            device_id=peer, device_id_type=MESH)
+        across.start()
+        emitted.append((own, across))
+
+    for phase in (2, 1, 0):
+        size = 256 // 4 ** phase
+        half = size // 2
+        base = bases[phase]
+        last = phase == 0
+
+        def part(c, by, upper):
+            axis = (c + phase) % 3
+            return base[c] + lax.rem(coord[axis] + by, side) * size + (half if upper else 0)
+
+        def spread(c, kind, start, upward):
+            axis = (c + phase) % 3
+            span = pl.ds(start, half)
+            copy = pltpu.make_async_remote_copy(
+                full.at[c, span], full.at[c, span], ag_send.at[c, phase, kind], ag_recv.at[c, phase, kind],
+                device_id=plus[axis] if upward else minus[axis], device_id_type=MESH)
+            copy.start()
+            sent.append(copy)
+            return copy
+
+        direct, passed = {}, {}
+        for c in range(colors):
+            low, high = part(c, 0, False), part(c, 0, True)
+            direct[c] = (spread(c, 0, low, True), spread(c, 1, high, False),
+                         spread(c, 2, high, True), spread(c, 3, low, False))
+            if last:
+                emit(c, 0, low, size)
+        for c in range(colors):
+            direct[c][0].wait_recv()
+            up = spread(c, 4, part(c, 3, False), True)
+            direct[c][1].wait_recv()
+            down = spread(c, 5, part(c, 1, True), False)
+            passed[c] = (up, down)
+            if last:
+                emit(c, 1, part(c, 3, False), half)
+                emit(c, 2, part(c, 1, True), half)
+        for c in range(colors):
+            direct[c][2].wait_recv()
+            if last:
+                emit(c, 3, part(c, 3, True), half)
+            direct[c][3].wait_recv()
+            if last:
+                emit(c, 4, part(c, 1, False), half)
+        for c in range(colors):
+            passed[c][0].wait_recv()
+            if last:
+                emit(c, 5, part(c, 2, False), half)
+            passed[c][1].wait_recv()
+            if last:
+                emit(c, 6, part(c, 2, True), half)
+
+    for copy in sent:
+        copy.wait_send()
+    for own, across in emitted:
+        own.wait()
+        across.wait()
+
+
+def reduce_all(grads, side):
+    colors = grads.shape[0]
+    hbm = pl.BlockSpec(memory_space=pl.ANY)
+    return pl.pallas_call(
+        functools.partial(reduce_kernel, side),
+        out_shape=jax.ShapeDtypeStruct((2 * colors, TILES, 8, 128), F32),
+        in_specs=[hbm],
+        out_specs=hbm,
+        scratch_shapes=[
+            pltpu.VMEM((colors, TILES, 8, 128), F32),
+            pltpu.VMEM((colors, TILES, 8, 128), F32),
+            pltpu.VMEM((colors, 2, 168, 8, 128), F32),
+            pltpu.VMEM((colors, 2, 336, 8, 128), F32),
+            pltpu.SemaphoreType.DMA((colors, 4)),
+            pltpu.SemaphoreType.DMA((colors, 3, 6)),
+            pltpu.SemaphoreType.DMA((colors, 3, 6)),
+            pltpu.SemaphoreType.DMA((colors, 3, 6)),
+            pltpu.SemaphoreType.DMA((colors, 3, 6)),
+            pltpu.SemaphoreType.DMA((colors, 7)),
+            pltpu.SemaphoreType.DMA((colors, 7)),
+            pltpu.SemaphoreType.DMA((colors, 7)),
+        ],
+        compiler_params=pltpu.CompilerParams(collective_id=2, has_side_effects=True,
+                                             vmem_limit_bytes=56 * 1024 * 1024),
+        name='reduce_all',
+    )(grads)
+
+
+def finish_kernel(terms, flat_ref, loss_ref, gw1_ref, gw2_ref, gg1_ref, gg2_ref, gproj_ref):
+    layer = pl.program_id(0)
+    inv = 1.0 / (terms * flat_ref[0, COUNT_TILE, 0:1, 0:1])
+    two = 2.0 * inv
+
+    def unpack(ref, start, rows):
+        width = ref.shape[2]
+        for ct in range(-(-width // 128)):
+            lanes = min(128, width - ct * 128)
+            piece = flat_ref[0, start + ct * ROW_TILES:start + (ct + 1) * ROW_TILES].reshape(rows, 128) * two
+            ref[0, :, ct * 128:ct * 128 + lanes] = piece[:, :lanes]
+
+    unpack(gproj_ref, 0, gproj_ref.shape[1])
+    unpack(gw2_ref, W2_AT, gw2_ref.shape[1])
+    unpack(gw1_ref, W1_AT, gw1_ref.shape[1])
+    for ref, start in ((gg1_ref, SMALL_AT), (gg2_ref, SMALL_AT + 3)):
+        width = ref.shape[1]
+        for ct in range(-(-width // 128)):
+            lanes = min(128, width - ct * 128)
+            cols = slice(ct * 128, ct * 128 + lanes)
+            row = flat_ref[0, start + ct, 0:1, 0:lanes] * two
+            here = lax.broadcasted_iota(jnp.int32, (ref.shape[0], lanes), 0) == layer
+            ref[:, cols] = jnp.where(here, row, ref[:, cols])
+
+    @pl.when(layer == 0)
+    def _():
+        loss_ref[...] = jnp.zeros_like(loss_ref)
+
+    loss_ref[...] += flat_ref[0, SQ_TILE, 0:1, 0:1] * inv
+
+
+def finish(flat, width, hidden, t_width):
+    layers = flat.shape[0]
+    per_layer = lambda a, b: pl.BlockSpec((1, a, b), lambda l: (l, 0, 0))
+    whole = lambda a, b: pl.BlockSpec((a, b), lambda l: (0, 0))
+    return pl.pallas_call(
+        functools.partial(finish_kernel, float(layers * t_width)),
+        grid=(layers,),
+        out_shape=(jax.ShapeDtypeStruct((1, 1), F32),
+                   jax.ShapeDtypeStruct((layers, width, hidden), F32),
+                   jax.ShapeDtypeStruct((layers, width, hidden), F32),
+                   jax.ShapeDtypeStruct((layers, width), F32),
+                   jax.ShapeDtypeStruct((layers, width), F32),
+                   jax.ShapeDtypeStruct((layers, width, t_width), F32)),
+        in_specs=[pl.BlockSpec((1, TILES, 8, 128), lambda l: (l, 0, 0, 0))],
+        out_specs=(whole(1, 1), per_layer(width, hidden), per_layer(width, hidden),
+                   whole(layers, width), whole(layers, width), per_layer(width, t_width)),
+        compiler_params=pltpu.CompilerParams(vmem_limit_bytes=48 * 1024 * 1024),
+        name='finish',
+    )(flat)
 
 
 def solution(mesh):
+    side = round(mesh.shape['data'] ** (1 / 3))
+
     def body(x_t, x_s, lengths, t_w1, t_w2, t_gain, s_w1, s_w2, s_gain1, s_gain2, s_proj):
-        n_feat = s_w1.shape[0]
-        feats = teacher(x_t, t_w1, t_w2, t_gain, n_feat)
-        gw1, gw2, gg1, gg2, gproj, sq = student(x_s, lengths, feats, s_w1, s_w2, s_gain1, s_gain2, s_proj)
-        tokens = jnp.sum(lengths).astype(F32)
-        gw1, gw2, gproj, gg1, gg2, sq, tokens = lax.psum((gw1, gw2, gproj, gg1, gg2, sq, tokens), ALL_AXES)
-        inv = 1.0 / (n_feat * x_t.shape[2] * tokens)
-        two = 2.0 * inv
-        shape = s_gain1.shape
-        return (sq[0, 0] * inv, gw1 * two, gw2 * two, gg1.reshape(shape) * two, gg2.reshape(shape) * two, gproj * two)
+        layers, width, hidden = s_w1.shape
+        feats = teacher(x_t, t_w1, t_w2, t_gain, layers)
+        grads = student(jnp.swapaxes(x_s, 1, 2), lengths, feats, s_w1, jnp.swapaxes(s_w2, 1, 2),
+                        s_gain1, s_gain2, s_proj)
+        flat = reduce_all(grads, side)
+        loss, gw1, gw2, gg1, gg2, gproj = finish(flat, width, hidden, x_t.shape[2])
+        return loss[0, 0], gw1, jnp.swapaxes(gw2, 1, 2), gg1, gg2, gproj
 
     in_specs = (P('data', 'model', None), P(ALL_AXES, None, None), P(ALL_AXES),
                 P(None, None, 'model'), P(None, 'model', None), P(), P(), P(), P(), P(), P())

time: 498 us -> 342 us (0.69)
  waiting for transfers between devices: 161 us -> 0 us
  Pallas kernels: 197 us -> 338 us
  blocking collectives: 70.6 us -> 0 us
  local copies, waits for them, and re-layouts: 29.1 us -> 2.84 us
  other arithmetic: 23 us -> 0 us
  between operations: 17.2 us -> 1.32 us
    psum x1 -> x0, waiting for transfers between devices: 161 us -> none  [body(): lax.psum((gw1, gw2, gproj, gg1, gg2, sq, tokens), ALL_AXES)]
    pallas_call x1 -> x3, Pallas kernels: 30.1 us -> 171 us  [the longest x1 120 us: reduce_all(): pl.pallas_call(functools.partial(reduce_kernel, side), out_shape=jax.Shap...]
    psum x1 -> x0, blocking collectives: 70.6 us -> none  [body(): lax.psum((gw1, gw2, gproj, gg1, gg2, sq, tokens), ALL_AXES)]
    mul x4 -> x0, other arithmetic: 23 us -> none  [the longest x1 9.34 us: body(): gw2 * two]
    unnamed x13 -> x6, local copies, waits for them, and re-layouts: 25.5 us -> 2.84 us
  transfers between devices with their start and end apart: 1 -> 0, of which waited for: 1 -> 0; matrix products, arithmetic and copies ran while one was open for 0% -> 0% of each run, Pallas kernels for 0% -> 0%
where the time goes in v2:
time: 342 us
  Pallas kernels  338 us (99%)
    pallas_call x1, Pallas kernels, teacher(): pl.pallas_call(functools.partial(teacher_kernel, layers, layers // n_feat...  167 us
    pallas_call x1, Pallas kernels, reduce_all(): pl.pallas_call(functools.partial(reduce_kernel, side), out_shape=jax.Shap...  120 us
    pallas_call x1, Pallas kernels, student(): pl.pallas_call(student_kernel, out_shape=jax.ShapeDtypeStruct((layers //...  33.8 us
    pallas_call x1, Pallas kernels, finish(): pl.pallas_call(functools.partial(finish_kernel, float(layers * t_width)),...  17.2 us

profile of v2, /device:TPU:1, one launch (start us, length us, event | category | flops | bytes accessed | tf_op | source)
XLA Modules:
  0.0 341.8 jit_solution(15341578738595086444)
XLA Ops:
  1.3 0.0 copy-start.1
  1.3 0.9 copy-done.1
  2.2 0.0 copy-start.2
  2.2 0.9 copy-done.2
  3.1 166.6 %teacher.1.feat_ref = bf16[6,128,768]{2,1,0:T(8,128)(2,1)S(1)} custom-call(bf16[2,64,768]{2,1,0:T(8,128)(2,1)S(1)} %copy-done.1, f32[48,768]{1,0:T(8,128)S(1)} %copy-done.2, bf16[48,768,1536]{2,1,0:T(8,128)(2,1)} %w1_hbm.1, bf16[48,1536,768]{2,1,0:T(8,128)(2,1)} %w2_hbm.1), custom_call_target="tpu_custom_call" | custom-call | flops 57982058496 | bytes 226492416 | tf_op jit(solution)/shard_map/teacher/pallas_call | solution.py:124
  169.7 0.0 copy-start
  169.7 1.0 copy-done
  170.7 33.8 %student.1.g_hbm = f32[3,1024,8,128]{3,2,1,0:T(8,128)} custom-call(s32[1]{0:T(128)S(6)} %copy.17.len_ref, bf16[1,312,128]{2,1,0:T(8,128)(2,1)} %bitcast.5, bf16[6,128,768]{2,1,0:T(8,128)(2,1)} %copy-done, bf16[6,312,1248]{2,1,0:T(8,128)(2,1)} %w1_ref.1, bf16[6,312,1248]{2,1,0:T(8,128)(2,1)} %bitcast.4, f32[6,312]{1,0:T(8,128)} %g1_ref.1, f32[6,312]{1,0:T(8,128)} %g2_ref.1, ...), custom_call_target="tpu_custom_call" | custom-call | tf_op jit(solution)/shard_map/student/pallas_call | solution.py:294
  204.5 120.1 %reduce_all.1.flat_ref = f32[6,1024,8,128]{3,2,1,0:T(8,128)} custom-call(f32[3,1024,8,128]{3,2,1,0:T(8,128)} %student.1.g_hbm), custom_call_target="tpu_custom_call" | custom-call | tf_op jit(solution)/shard_map/reduce_all/pallas_call | solution.py:480
  324.6 17.2 %finish.1 = (f32[1,1]{1,0:T(1,128)}, f32[6,312,1248]{2,1,0:T(8,128)}, f32[6,312,1248]{2,1,0:T(8,128)}, f32[6,312]{1,0:T(8,128)}, f32[6,312]{1,0:T(8,128)}, /*index=5*/f32[6,312,768]{2,1,0:T(8,128)}) custom-call(f32[6,1024,8,128]{3,2,1,0:T(8,128)} %reduce_all.1.flat_ref), custom_call_target="tpu_custom_call" | custom-call | tf_op jit(solution)/shard_map/finish/pallas_call | solution.py:540
Async XLA Ops:
  1.3 0.9 copy-start.1
  2.2 0.9 copy-start.2
  169.7 1.0 copy-start

commit v3 on v2

--- a/solution.py
+++ b/solution.py
@@ -17,7 +17,8 @@
 
 
 def gelu(x):
-    return x * (0.5 * (1.0 + jnp.tanh(GELU_C * (x + GELU_A * (x * x * x)))))
+    half = 0.5 * x
+    return half + half * jnp.tanh(x * (GELU_C + (GELU_C * GELU_A) * (x * x)))
 
 
 def gelu_grad(x):
@@ -30,17 +31,15 @@
     return lax.rsqrt(jnp.mean(wide * wide, axis=-1, keepdims=True) + RMS_EPS)
 
 
-def teacher_kernel(layers, per_group, x_ref, gain_ref, w1_hbm, w2_hbm, feat_ref,
-                   xbuf, hbuf, ubuf, part, recv, w1buf, w2buf,
+def teacher_kernel(layers, per_group, spans, k_chunks, x_ref, gain_ref, w1_hbm, w2_hbm, feat_ref,
+                   xbuf, hbuf, part, recv, w1buf, w2buf,
                    x_send, x_recv, w_sem, p_send, p_recv):
     core = lax.axis_index('model')
     peer = {'model': 1 - core}
     seqs, pos, width = hbuf.shape
-    hidden = ubuf.shape[1]
-    n_out = part.shape[1]
-    out_w = part.shape[3]
-    slots = w1buf.shape[0]
-    half = hidden // 3
+    slots, _, hidden = w1buf.shape
+    blocks, out_w = part.shape[1], part.shape[3]
+    step = hidden // k_chunks
 
     def fetch(layer, slot):
         return (pltpu.make_async_copy(w1_hbm.at[layer], w1buf.at[slot], w_sem.at[slot, 0]),
@@ -52,27 +51,29 @@
 
     barrier = pltpu.get_barrier_semaphore()
     pl.semaphore_signal(barrier, inc=1, device_id=peer, device_id_type=MESH)
+    part[...] = jnp.zeros(part.shape, F32)
+    recv[1] = jnp.zeros(recv.shape[1:], F32)
+    xbuf[core] = x_ref[...]
     pl.semaphore_wait(barrier, 1)
 
     x_copy = pltpu.make_async_remote_copy(x_ref, xbuf.at[core], x_send, x_recv, device_id=peer, device_id_type=MESH)
     x_copy.start()
-    xbuf[core] = x_ref[...]
     x_copy.wait()
     for seq in range(seqs):
         for c in range(2):
             hbuf[seq, c * (pos // 2):(c + 1) * (pos // 2), :] = xbuf[c, seq]
 
-    def exchange(seq, slot, c):
+    def exchange(seq, slot, k):
+        span = pl.ds(*spans[k])
         return pltpu.make_async_remote_copy(
-            part.at[seq, c], recv.at[slot, seq, c], p_send.at[seq, c], p_recv.at[slot, seq, c],
+            part.at[seq, span], recv.at[slot, seq, span], p_send.at[seq, k], p_recv.at[slot, seq, k],
             device_id=peer, device_id_type=MESH)
 
     def absorb(seq, slot):
-        for c in range(n_out):
-            exchange(seq, slot, c).wait()
-            cols = slice(c * out_w, (c + 1) * out_w)
-            update = part[seq, c] + recv[slot, seq, c]
-            hbuf[seq, :, cols] = (hbuf[seq, :, cols].astype(F32) + update).astype(BF16)
+        update = jnp.concatenate([part[seq, b] + recv[slot, seq, b] for b in range(blocks)], axis=1)
+        state = (hbuf[seq].astype(F32) + update).astype(BF16)
+        hbuf[seq] = state
+        return state.astype(F32)
 
     def block(layer, _):
         slot = lax.rem(layer, slots)
@@ -82,25 +83,31 @@
             for copy in fetch(layer + (slots - 1), lax.rem(layer + (slots - 1), slots)):
                 copy.start()
 
-        fetched = fetch(layer, slot)
         for seq in range(seqs):
+            old = lax.rem(layer + 1, 2)
+            if seq == 0:
+                for copy in fetch(layer, slot):
+                    copy.wait()
+
             @pl.when(layer > 0)
             def _():
-                absorb(seq, lax.rem(layer + 1, 2))
-            if seq == 0:
-                fetched[0].wait()
-            wide = hbuf[seq].astype(F32)
+                for k in range(len(spans)):
+                    exchange(seq, old, k).wait()
+
+            wide = absorb(seq, old)
             normed = (wide * inv_rms(wide) * gain_ref[pl.ds(layer, 1), :]).astype(BF16)
-            for c in range(3):
-                cols = slice(c * half, (c + 1) * half)
-                pre = jnp.dot(normed, w1buf[slot, :, cols], preferred_element_type=F32)
-                ubuf[:, cols] = gelu(pre).astype(BF16)
-            if seq == 0:
-                fetched[1].wait()
-            act = ubuf[...]
-            for c in range(n_out):
-                part[seq, c] = jnp.dot(act, w2buf[slot, :, c * out_w:(c + 1) * out_w], preferred_element_type=F32)
-                exchange(seq, lax.rem(layer, 2), c).start()
+            acc = [None] * len(spans)
+            for c in range(k_chunks):
+                pre = jnp.dot(normed, w1buf[slot, :, c * step:(c + 1) * step], preferred_element_type=F32)
+                act = gelu(pre).astype(BF16)
+                for k, (first, count) in enumerate(spans):
+                    cols = slice(first * out_w, (first + count) * out_w)
+                    term = jnp.dot(act, w2buf[slot, c * step:(c + 1) * step, cols], preferred_element_type=F32)
+                    acc[k] = term if acc[k] is None else acc[k] + term
+                    if c == k_chunks - 1:
+                        for b in range(count):
+                            part[seq, first + b] = acc[k][:, b * out_w:(b + 1) * out_w]
+                        exchange(seq, lax.rem(layer, 2), k).start()
 
         @pl.when((layer > 0) & (lax.rem(layer, per_group) == 0))
         def _():
@@ -109,6 +116,8 @@
 
     lax.fori_loop(0, layers, block, 0)
     for seq in range(seqs):
+        for k in range(len(spans)):
+            exchange(seq, (layers - 1) % 2, k).wait()
         absorb(seq, (layers - 1) % 2)
     feat_ref[layers // per_group - 1] = hbuf[core]
 
@@ -117,28 +126,28 @@
     layers, width, hidden = t_w1.shape
     seqs, half_pos, _ = x_t.shape
     pos = 2 * half_pos
-    slots, n_out = 3, 3
-    out_w = width // n_out
+    slots, blocks = 3, 3
+    out_w = width // blocks
+    spans = ((0, 1), (1, 2))
     vmem = pl.BlockSpec(memory_space=pltpu.VMEM)
     hbm = pl.BlockSpec(memory_space=pl.ANY)
     return pl.pallas_call(
-        functools.partial(teacher_kernel, layers, layers // n_feat),
+        functools.partial(teacher_kernel, layers, layers // n_feat, spans, 1),
         out_shape=jax.ShapeDtypeStruct((n_feat, pos, width), BF16),
         in_specs=[vmem, vmem, hbm, hbm],
         out_specs=vmem,
         scratch_shapes=[
             pltpu.VMEM((2, seqs, half_pos, width), BF16),
             pltpu.VMEM((seqs, pos, width), BF16),
-            pltpu.VMEM((pos, hidden), BF16),
-            pltpu.VMEM((seqs, n_out, pos, out_w), F32),
-            pltpu.VMEM((2, seqs, n_out, pos, out_w), F32),
+            pltpu.VMEM((seqs, blocks, pos, out_w), F32),
+            pltpu.VMEM((2, seqs, blocks, pos, out_w), F32),
             pltpu.VMEM((slots, width, hidden), BF16),
             pltpu.VMEM((slots, hidden, width), BF16),
             pltpu.SemaphoreType.DMA,
             pltpu.SemaphoreType.DMA,
             pltpu.SemaphoreType.DMA((slots, 2)),
-            pltpu.SemaphoreType.DMA((seqs, n_out)),
-            pltpu.SemaphoreType.DMA((2, seqs, n_out)),
+            pltpu.SemaphoreType.DMA((seqs, len(spans))),
+            pltpu.SemaphoreType.DMA((2, seqs, len(spans))),
         ],
         compiler_params=pltpu.CompilerParams(collective_id=0, has_side_effects=True,
                                              vmem_limit_bytes=40 * 1024 * 1024),
@@ -314,12 +323,19 @@
     )(lengths, x_s, feats, s_w1, s_w2t, s_gain1, s_gain2, s_proj)
 
 
+SUBS = 2
+ORDER = ((0, 0), (0, 1), (1, 0), (0, 2), (1, 1), (0, 3), (1, 2), (0, 4), (1, 3), (0, 5), (1, 4), (0, 6), (1, 5), (0, 7),
+         (1, 6), (0, 8), (1, 7), (0, 9), (1, 8), (0, 10), (1, 9), (0, 11), (1, 10), (0, 12), (1, 11), (0, 13), (1, 12),
+         (1, 13))
+
+
 def reduce_kernel(side, g_hbm, out_hbm, data, full, near, far,
                   load_sem, rs_send, rs_recv, ag_send, ag_recv, own_sem, d2d_send, d2d_recv):
     core = lax.axis_index('model')
     chip = lax.axis_index('data')
     peer = {'model': 1 - core}
     colors = data.shape[0]
+    sub_tiles = TILES // SUBS
     coord = [lax.rem(chip, side), lax.rem(lax.div(chip, side), side), lax.div(chip, side * side)]
 
     def shifted(axis, by):
@@ -327,13 +343,13 @@
         moved[axis] = lax.rem(coord[axis] + by, side)
         return {'data': (moved[2] * side + moved[1]) * side + moved[0]}
 
-    def load(c, a):
-        span = pl.ds(a * 256, 256)
-        return pltpu.make_async_copy(g_hbm.at[c, span], data.at[c, span], load_sem.at[c, a])
-
-    for a in range(4):
+    def load(c, sub):
+        span = pl.ds(sub * sub_tiles, sub_tiles)
+        return pltpu.make_async_copy(g_hbm.at[c, span], data.at[c, span], load_sem.at[c, sub])
+
+    for sub in range(SUBS):
         for c in range(colors):
-            load(c, a).start()
+            load(c, sub).start()
 
     barrier = pltpu.get_barrier_semaphore()
     pl.semaphore_signal(barrier, inc=1, device_id=peer, device_id_type=MESH)
@@ -342,130 +358,123 @@
             pl.semaphore_signal(barrier, inc=1, device_id=shifted(axis, by), device_id_type=MESH)
     pl.semaphore_wait(barrier, 7)
 
-    for a in range(4):
-        for c in range(colors):
-            load(c, a).wait()
-
     plus = [shifted(axis, 1) for axis in range(3)]
     minus = [shifted(axis, side - 1) for axis in range(3)]
     sent = []
-    base = [0] * colors
-    bases = []
-    near_at, far_at = 0, 0
-    size = 256
-
-    for phase in range(3):
-        half = size // 2
-        bases.append(list(base))
-
-        def chunk(c, by):
-            axis = (c + phase) % 3
-            return base[c] + lax.rem(coord[axis] + by, side) * size
-
-        def push(c, kind, src, dst, upward):
-            axis = (c + phase) % 3
-            copy = pltpu.make_async_remote_copy(
-                src, dst, rs_send.at[c, phase, kind], rs_recv.at[c, phase, kind],
-                device_id=plus[axis] if upward else minus[axis], device_id_type=MESH)
-            copy.start()
-            sent.append(copy)
-            return copy
-
-        first, early, late = {}, {}, {}
-        for c in range(colors):
-            opp, nxt, prv = chunk(c, 2), chunk(c, 1), chunk(c, 3)
-            first[c] = (
-                push(c, 0, data.at[c, pl.ds(opp, half)], near.at[c, 0, pl.ds(near_at, half)], True),
-                push(c, 1, data.at[c, pl.ds(opp + half, half)], near.at[c, 1, pl.ds(near_at, half)], False))
-            early[c] = (
-                push(c, 2, data.at[c, pl.ds(nxt + half, half)], far.at[c, 0, pl.ds(far_at + half, half)], True),
-                push(c, 3, data.at[c, pl.ds(prv, half)], far.at[c, 1, pl.ds(far_at, half)], False))
-        for c in range(colors):
-            nxt, prv = chunk(c, 1), chunk(c, 3)
-            first[c][0].wait_recv()
-            span = pl.ds(nxt, half)
-            data[c, span] = data[c, span] + near[c, 0, pl.ds(near_at, half)]
-            up = push(c, 4, data.at[c, span], far.at[c, 0, pl.ds(far_at, half)], True)
-            first[c][1].wait_recv()
-            span = pl.ds(prv + half, half)
-            data[c, span] = data[c, span] + near[c, 1, pl.ds(near_at, half)]
-            down = push(c, 5, data.at[c, span], far.at[c, 1, pl.ds(far_at + half, half)], False)
-            late[c] = (up, down)
-        for c in range(colors):
-            for copy in early[c] + late[c]:
-                copy.wait_recv()
-            mine = pl.ds(chunk(c, 0), size)
-            both = far[c, 0, pl.ds(far_at, size)] + far[c, 1, pl.ds(far_at, size)]
-            if phase < 2:
-                data[c, mine] = data[c, mine] + both
-            else:
-                full[c, mine] = data[c, mine] + both
-        base = [chunk(c, 0) for c in range(colors)]
-        near_at, far_at, size = near_at + half, far_at + size, half // 2
-
     emitted = []
 
-    def emit(c, slot, start, count):
+    def remote(src, dst, send_sem, recv_sem, axis, upward):
+        copy = pltpu.make_async_remote_copy(src, dst, send_sem, recv_sem,
+                                            device_id=plus[axis] if upward else minus[axis], device_id_type=MESH)
+        copy.start()
+        sent.append(copy)
+        return copy
+
+    def emit(c, sub, slot, start, count):
         layer = 2 * c + core
         span = pl.ds(start, count)
-        own = pltpu.make_async_copy(full.at[c, span], out_hbm.at[layer, span], own_sem.at[c, slot])
+        k = sub * 7 + slot
+        own = pltpu.make_async_copy(full.at[c, span], out_hbm.at[layer, span], own_sem.at[c, k])
         own.start()
         across = pltpu.make_async_remote_copy(
-            full.at[c, span], out_hbm.at[layer, span], d2d_send.at[c, slot], d2d_recv.at[c, slot],
+            full.at[c, span], out_hbm.at[layer, span], d2d_send.at[c, k], d2d_recv.at[c, k],
             device_id=peer, device_id_type=MESH)
         across.start()
         emitted.append((own, across))
 
-    for phase in (2, 1, 0):
-        size = 256 // 4 ** phase
-        half = size // 2
-        base = bases[phase]
-        last = phase == 0
-
-        def part(c, by, upper):
+    def stream(c, sub):
+        load(c, sub).wait()
+        base = sub * sub_tiles
+        bases = []
+        near_at, far_at = sub * (near.shape[2] // SUBS), sub * (far.shape[2] // SUBS)
+        size = sub_tiles // side
+        for phase in range(3):
+            half = size // 2
             axis = (c + phase) % 3
-            return base[c] + lax.rem(coord[axis] + by, side) * size + (half if upper else 0)
-
-        def spread(c, kind, start, upward):
+            bases.append(base)
+
+            def chunk(by):
+                return base + lax.rem(coord[axis] + by, side) * size
+
+            def push(kind, src, dst, upward):
+                k = sub * 6 + kind
+                return remote(src, dst, rs_send.at[c, phase, k], rs_recv.at[c, phase, k], axis, upward)
+
+            opp, nxt, prv, mine = chunk(2), chunk(1), chunk(3), chunk(0)
+            near_span, far_low = pl.ds(near_at, half), pl.ds(far_at, half)
+            far_high, far_all = pl.ds(far_at + half, half), pl.ds(far_at, size)
+            first_up = push(0, data.at[c, pl.ds(opp, half)], near.at[c, 0, near_span], True)
+            first_down = push(1, data.at[c, pl.ds(opp + half, half)], near.at[c, 1, near_span], False)
+            early_up = push(2, data.at[c, pl.ds(nxt + half, half)], far.at[c, 0, far_high], True)
+            early_down = push(3, data.at[c, pl.ds(prv, half)], far.at[c, 1, far_low], False)
+            yield
+            first_up.wait_recv()
+            span = pl.ds(nxt, half)
+            data[c, span] = data[c, span] + near[c, 0, near_span]
+            late_up = push(4, data.at[c, span], far.at[c, 0, far_low], True)
+            first_down.wait_recv()
+            span = pl.ds(prv + half, half)
+            data[c, span] = data[c, span] + near[c, 1, near_span]
+            late_down = push(5, data.at[c, span], far.at[c, 1, far_high], False)
+            yield
+            for copy in (early_up, early_down, late_up, late_down):
+                copy.wait_recv()
+            mine_span = pl.ds(mine, size)
+            both = far[c, 0, far_all] + far[c, 1, far_all]
+            if phase < 2:
+                data[c, mine_span] = data[c, mine_span] + both
+            else:
+                full[c, mine_span] = data[c, mine_span] + both
+            base = mine
+            near_at, far_at, size = near_at + half, far_at + size, size // side
+
+        for phase in (2, 1, 0):
+            size = sub_tiles // side ** (phase + 1)
+            half = size // 2
             axis = (c + phase) % 3
-            span = pl.ds(start, half)
-            copy = pltpu.make_async_remote_copy(
-                full.at[c, span], full.at[c, span], ag_send.at[c, phase, kind], ag_recv.at[c, phase, kind],
-                device_id=plus[axis] if upward else minus[axis], device_id_type=MESH)
-            copy.start()
-            sent.append(copy)
-            return copy
-
-        direct, passed = {}, {}
-        for c in range(colors):
-            low, high = part(c, 0, False), part(c, 0, True)
-            direct[c] = (spread(c, 0, low, True), spread(c, 1, high, False),
-                         spread(c, 2, high, True), spread(c, 3, low, False))
+            base = bases[phase]
+            last = phase == 0
+
+            def part(by, upper):
+                return base + lax.rem(coord[axis] + by, side) * size + (half if upper else 0)
+
+            def spread(kind, start, upward):
+                k = sub * 6 + kind
+                span = pl.ds(start, half)
+                return remote(full.at[c, span], full.at[c, span], ag_send.at[c, phase, k], ag_recv.at[c, phase, k],
+                              axis, upward)
+
+            low, high = part(0, False), part(0, True)
+            direct = (spread(0, low, True), spread(1, high, False), spread(2, high, True), spread(3, low, False))
             if last:
-                emit(c, 0, low, size)
-        for c in range(colors):
-            direct[c][0].wait_recv()
-            up = spread(c, 4, part(c, 3, False), True)
-            direct[c][1].wait_recv()
-            down = spread(c, 5, part(c, 1, True), False)
-            passed[c] = (up, down)
+                emit(c, sub, 0, low, size)
+            yield
+            direct[0].wait_recv()
+            up = spread(4, part(3, False), True)
+            direct[1].wait_recv()
+            down = spread(5, part(1, True), False)
             if last:
-                emit(c, 1, part(c, 3, False), half)
-                emit(c, 2, part(c, 1, True), half)
-        for c in range(colors):
-            direct[c][2].wait_recv()
+                emit(c, sub, 1, part(3, False), half)
+                emit(c, sub, 2, part(1, True), half)
+            yield
+            direct[2].wait_recv()
             if last:
-                emit(c, 3, part(c, 3, True), half)
-            direct[c][3].wait_recv()
+                emit(c, sub, 3, part(3, True), half)
+            direct[3].wait_recv()
             if last:
-                emit(c, 4, part(c, 1, False), half)
-        for c in range(colors):
-            passed[c][0].wait_recv()
+                emit(c, sub, 4, part(1, False), half)
+                yield
+            up.wait_recv()
             if last:
-                emit(c, 5, part(c, 2, False), half)
-            passed[c][1].wait_recv()
+                emit(c, sub, 5, part(2, False), half)
+            down.wait_recv()
             if last:
-                emit(c, 6, part(c, 2, True), half)
+                emit(c, sub, 6, part(2, True), half)
+
+    streams = [[stream(c, sub) for c in range(colors)] for sub in range(SUBS)]
+    for sub, _ in ORDER:
+        for one in streams[sub]:
+            next(one, None)
 
     for copy in sent:
         copy.wait_send()
@@ -487,14 +496,14 @@
             pltpu.VMEM((colors, TILES, 8, 128), F32),
             pltpu.VMEM((colors, 2, 168, 8, 128), F32),
             pltpu.VMEM((colors, 2, 336, 8, 128), F32),
-            pltpu.SemaphoreType.DMA((colors, 4)),
-            pltpu.SemaphoreType.DMA((colors, 3, 6)),
-            pltpu.SemaphoreType.DMA((colors, 3, 6)),
-            pltpu.SemaphoreType.DMA((colors, 3, 6)),
-            pltpu.SemaphoreType.DMA((colors, 3, 6)),
-            pltpu.SemaphoreType.DMA((colors, 7)),
-            pltpu.SemaphoreType.DMA((colors, 7)),
-            pltpu.SemaphoreType.DMA((colors, 7)),
+            pltpu.SemaphoreType.DMA((colors, SUBS)),
+            pltpu.SemaphoreType.DMA((colors, 3, 6 * SUBS)),
+            pltpu.SemaphoreType.DMA((colors, 3, 6 * SUBS)),
+            pltpu.SemaphoreType.DMA((colors, 3, 6 * SUBS)),
+            pltpu.SemaphoreType.DMA((colors, 3, 6 * SUBS)),
+            pltpu.SemaphoreType.DMA((colors, 7 * SUBS)),
+            pltpu.SemaphoreType.DMA((colors, 7 * SUBS)),
+            pltpu.SemaphoreType.DMA((colors, 7 * SUBS)),
         ],
         compiler_params=pltpu.CompilerParams(collective_id=2, has_side_effects=True,
                                              vmem_limit_bytes=56 * 1024 * 1024),

time: 342 us -> 297 us (0.87)
  Pallas kernels: 338 us -> 293 us
    pallas_call x1, Pallas kernels: 167 us -> 127 us  [teacher(): pl.pallas_call(functools.partial(teacher_kernel, layers, layers // n_feat...]
    pallas_call x1, Pallas kernels: 120 us -> 115 us  [reduce_all(): pl.pallas_call(functools.partial(reduce_kernel, side), out_shape=jax.Shap...]
where the time goes in v3:
time: 297 us
  Pallas kernels  293 us (99%)
    pallas_call x1, Pallas kernels, teacher(): pl.pallas_call(functools.partial(teacher_kernel, layers, layers // n_feat...  127 us
    pallas_call x1, Pallas kernels, reduce_all(): pl.pallas_call(functools.partial(reduce_kernel, side), out_shape=jax.Shap...  115 us
    pallas_call x1, Pallas kernels, student(): pl.pallas_call(student_kernel, out_shape=jax.ShapeDtypeStruct((layers //...  34 us
    pallas_call x1, Pallas kernels, finish(): pl.pallas_call(functools.partial(finish_kernel, float(layers * t_width)),...  17.2 us

profile of v3, /device:TPU:1, one launch (start us, length us, event | category | flops | bytes accessed | tf_op | source)
XLA Modules:
  0.0 297.0 jit_solution(18390559173277678780)
XLA Ops:
  1.3 0.0 copy-start.1
  1.3 0.9 copy-done.1
  2.2 0.0 copy-start.2
  2.2 0.9 copy-done.2
  3.1 126.8 %teacher.1.feat_ref = bf16[6,128,768]{2,1,0:T(8,128)(2,1)S(1)} custom-call(bf16[2,64,768]{2,1,0:T(8,128)(2,1)S(1)} %copy-done.1, f32[48,768]{1,0:T(8,128)S(1)} %copy-done.2, bf16[48,768,1536]{2,1,0:T(8,128)(2,1)} %w1_hbm.1, bf16[48,1536,768]{2,1,0:T(8,128)(2,1)} %w2_hbm.1), custom_call_target="tpu_custom_call" | custom-call | flops 57982058496 | bytes 226492416 | tf_op jit(solution)/shard_map/teacher/pallas_call | solution.py:134
  129.9 0.0 copy-start
  129.9 1.0 copy-done
  131.0 34.0 %student.1.g_hbm = f32[3,1024,8,128]{3,2,1,0:T(8,128)} custom-call(s32[1]{0:T(128)S(6)} %copy.17.len_ref, bf16[1,312,128]{2,1,0:T(8,128)(2,1)} %bitcast.5, bf16[6,128,768]{2,1,0:T(8,128)(2,1)} %copy-done, bf16[6,312,1248]{2,1,0:T(8,128)(2,1)} %w1_ref.1, bf16[6,312,1248]{2,1,0:T(8,128)(2,1)} %bitcast.4, f32[6,312]{1,0:T(8,128)} %g1_ref.1, f32[6,312]{1,0:T(8,128)} %g2_ref.1, ...), custom_call_target="tpu_custom_call" | custom-call | tf_op jit(solution)/shard_map/student/pallas_call | solution.py:303
  165.0 114.9 %reduce_all.1.flat_ref = f32[6,1024,8,128]{3,2,1,0:T(8,128)} custom-call(f32[3,1024,8,128]{3,2,1,0:T(8,128)} %student.1.g_hbm), custom_call_target="tpu_custom_call" | custom-call | tf_op jit(solution)/shard_map/reduce_all/pallas_call | solution.py:489
  279.9 17.2 %finish.1 = (f32[1,1]{1,0:T(1,128)}, f32[6,312,1248]{2,1,0:T(8,128)}, f32[6,312,1248]{2,1,0:T(8,128)}, f32[6,312]{1,0:T(8,128)}, f32[6,312]{1,0:T(8,128)}, /*index=5*/f32[6,312,768]{2,1,0:T(8,128)}) custom-call(f32[6,1024,8,128]{3,2,1,0:T(8,128)} %reduce_all.1.flat_ref), custom_call_target="tpu_custom_call" | custom-call | tf_op jit(solution)/shard_map/finish/pallas_call | solution.py:549
Async XLA Ops:
  1.3 0.9 copy-start.1
  2.2 0.9 copy-start.2
  129.9 1.0 copy-start

commit v4 on v3

--- a/solution.py
+++ b/solution.py
@@ -200,11 +200,21 @@
         ref[idx, start + ct] = jnp.broadcast_to(piece, (8, 128))
 
 
-def student_kernel(len_ref, x_ref, feat_ref, w1_ref, w2_ref, g1_ref, g2_ref, proj_ref, out_hbm,
-                   grad, recv, s_in, normed_s, pre_s, act_s, dproj_s, send_sem, recv_sem, out_sem):
+def student_kernel(len_ref, x_ref, g1_ref, g2_ref, feat_hbm, w1_hbm, w2_hbm, proj_hbm, out_hbm,
+                   grad, recv, s_in, normed_s, pre_s, act_s, dproj_s, feat_ref, w1_ref, w2_ref, proj_ref,
+                   in_sem, send_sem, recv_sem, out_sem):
     core = lax.axis_index('model')
     peer = {'model': 1 - core}
     layers = w1_ref.shape[0]
+
+    def fetch(layer):
+        pairs_of = ((w1_hbm, w1_ref), (w2_hbm, w2_ref), (proj_hbm, proj_ref), (feat_hbm, feat_ref))
+        return [pltpu.make_async_copy(src.at[layer], dst.at[layer], in_sem.at[layer, k])
+                for k, (src, dst) in enumerate(pairs_of)]
+
+    for layer in range(layers):
+        for copy in fetch(layer):
+            copy.start()
     pairs = layers // 2
     pos = x_ref.shape[2]
     barrier = pltpu.get_barrier_semaphore()
@@ -226,6 +236,8 @@
 
     def forward(layer, state):
         pair, mine, idx = place(layer)
+        for copy in fetch(layer):
+            copy.wait()
         s_in[layer] = state
         normed = (state * inv_rms(state) * g1_ref[pl.ds(layer, 1), :]).astype(BF16)
         normed_s[layer] = normed
@@ -280,8 +292,9 @@
 
     lax.fori_loop(0, layers, backward, jnp.zeros(s_in.shape[1:], F32))
 
-    def out_copy(pair):
-        return pltpu.make_async_copy(grad.at[pair], out_hbm.at[pair], out_sem.at[pair])
+    def out_copy(pair, part):
+        span = pl.ds(*PARTS[part])
+        return pltpu.make_async_copy(grad.at[pair, span], out_hbm.at[pair, span], out_sem.at[pair, part])
 
     for pair in reversed(range(pairs)):
         for part in range(3):
@@ -289,11 +302,11 @@
             start, size = PARTS[part]
             span = pl.ds(start, size)
             grad[pair, span] = grad[pair, span] + recv[pair, span]
-        out_copy(pair).start()
+            out_copy(pair, part).start()
     for pair in range(pairs):
         for part in range(3):
             send(pair, part).wait_send()
-        out_copy(pair).wait()
+            out_copy(pair, part).wait()
 
 
 def student(x_s, lengths, feats, s_w1, s_w2t, s_gain1, s_gain2, s_proj):
@@ -303,7 +316,7 @@
     return pl.pallas_call(
         student_kernel,
         out_shape=jax.ShapeDtypeStruct((layers // 2, TILES, 8, 128), F32),
-        in_specs=[pl.BlockSpec(memory_space=pltpu.SMEM)] + [vmem] * 7,
+        in_specs=[pl.BlockSpec(memory_space=pltpu.SMEM)] + [vmem] * 3 + [pl.BlockSpec(memory_space=pl.ANY)] * 4,
         out_specs=pl.BlockSpec(memory_space=pl.ANY),
         scratch_shapes=[
             pltpu.VMEM((layers, TILES, 8, 128), F32),
@@ -313,14 +326,19 @@
             pltpu.VMEM((layers, pos, hidden), F32),
             pltpu.VMEM((layers, pos, hidden), BF16),
             pltpu.VMEM((layers, pos, width), F32),
+            pltpu.VMEM(feats.shape, BF16),
+            pltpu.VMEM(s_w1.shape, BF16),
+            pltpu.VMEM(s_w2t.shape, BF16),
+            pltpu.VMEM(s_proj.shape, BF16),
+            pltpu.SemaphoreType.DMA((layers, 4)),
             pltpu.SemaphoreType.DMA((layers // 2, 3)),
             pltpu.SemaphoreType.DMA((layers // 2, 3)),
-            pltpu.SemaphoreType.DMA((layers // 2,)),
+            pltpu.SemaphoreType.DMA((layers // 2, 3)),
         ],
         compiler_params=pltpu.CompilerParams(collective_id=1, has_side_effects=True,
                                              vmem_limit_bytes=67_043_328),
         name='student',
-    )(lengths, x_s, feats, s_w1, s_w2t, s_gain1, s_gain2, s_proj)
+    )(lengths, x_s, s_gain1, s_gain2, feats, s_w1, s_w2t, s_proj)
 
 
 SUBS = 2

time: 297 us -> 294 us (0.990)
  Pallas kernels: 293 us -> 289 us
    pallas_call x1, Pallas kernels: 34 us -> 30.6 us  [student(): pl.pallas_call(student_kernel, out_shape=jax.ShapeDtypeStruct((layers //...]
where the time goes in v4:
time: 294 us
  Pallas kernels  289 us (98%)
    pallas_call x1, Pallas kernels, teacher(): pl.pallas_call(functools.partial(teacher_kernel, layers, layers // n_feat...  127 us
    pallas_call x1, Pallas kernels, reduce_all(): pl.pallas_call(functools.partial(reduce_kernel, side), out_shape=jax.Shap...  115 us
    pallas_call x1, Pallas kernels, student(): pl.pallas_call(student_kernel, out_shape=jax.ShapeDtypeStruct((layers //...  30.6 us
    pallas_call x1, Pallas kernels, finish(): pl.pallas_call(functools.partial(finish_kernel, float(layers * t_width)),...  17.2 us

profile of v4, /device:TPU:1, one launch (start us, length us, event | category | flops | bytes accessed | tf_op | source)
XLA Modules:
  0.0 293.6 jit_solution(5294186741913740835)
XLA Ops:
  1.3 0.0 copy-start.1
  1.3 0.9 copy-done.1
  2.2 0.0 copy-start.2
  2.2 0.9 copy-done.2
  3.1 126.8 %teacher.1.feat_hbm = bf16[6,128,768]{2,1,0:T(8,128)(2,1)S(1)} custom-call(bf16[2,64,768]{2,1,0:T(8,128)(2,1)S(1)} %copy-done.1, f32[48,768]{1,0:T(8,128)S(1)} %copy-done.2, bf16[48,768,1536]{2,1,0:T(8,128)(2,1)} %w1_hbm.2, bf16[48,1536,768]{2,1,0:T(8,128)(2,1)} %w2_hbm.1), custom_call_target="tpu_custom_call" | custom-call | flops 57982058496 | bytes 226492416 | tf_op jit(solution)/shard_map/teacher/pallas_call | solution.py:134
  129.9 0.0 copy-start
  129.9 1.0 copy-done
  131.0 30.6 %student.1.g_hbm = f32[3,1024,8,128]{3,2,1,0:T(8,128)} custom-call(s32[1]{0:T(128)S(6)} %copy.17.len_ref, bf16[1,312,128]{2,1,0:T(8,128)(2,1)} %bitcast.5, f32[6,312]{1,0:T(8,128)} %g1_ref.1, f32[6,312]{1,0:T(8,128)} %g2_ref.1, bf16[6,128,768]{2,1,0:T(8,128)(2,1)} %copy-done, bf16[6,312,1248]{2,1,0:T(8,128)(2,1)} %w1_hbm.3, bf16[6,312,1248]{2,1,0:T(8,128)(2,1)} %bitcast.4, ...), custom_call_target="tpu_custom_call" | custom-call | tf_op jit(solution)/shard_map/student/pallas_call | solution.py:316
  161.6 114.9 %reduce_all.1.flat_ref = f32[6,1024,8,128]{3,2,1,0:T(8,128)} custom-call(f32[3,1024,8,128]{3,2,1,0:T(8,128)} %student.1.g_hbm), custom_call_target="tpu_custom_call" | custom-call | tf_op jit(solution)/shard_map/reduce_all/pallas_call | solution.py:507
  276.5 17.2 %finish.1 = (f32[1,1]{1,0:T(1,128)}, f32[6,312,1248]{2,1,0:T(8,128)}, f32[6,312,1248]{2,1,0:T(8,128)}, f32[6,312]{1,0:T(8,128)}, f32[6,312]{1,0:T(8,128)}, /*index=5*/f32[6,312,768]{2,1,0:T(8,128)}) custom-call(f32[6,1024,8,128]{3,2,1,0:T(8,128)} %reduce_all.1.flat_ref), custom_call_target="tpu_custom_call" | custom-call | tf_op jit(solution)/shard_map/finish/pallas_call | solution.py:567
Async XLA Ops:
  1.3 0.9 copy-start.1
  2.2 0.9 copy-start.2
  129.9 1.0 copy-start
